TPU v7x, 32 devices: a whole 2x2x4 slice. The times are simulated.
32 devices in a mesh: ep: 8 (over y, x, core), dp: 4 (over z).
Axes of the slice: x: 2, y: 2, z: 4, core: 2. Of those that a mesh axis runs over, the one named last changes fastest.
Arguments:
- master_weights: float32 [8, 1024, 3584], P('ep', 'dp'), may hold values from -6 to 6
- first_moment: float32 [8, 1024, 3584], P('ep', 'dp'), may hold values from -6 to 6
- second_moment: float32 [8, 1024, 3584], P('ep', 'dp'), may hold values from 0.01 to 4
- expert_ids: int32 [8], replicated, may hold values from 0 to 255, as said below
- bucket_offsets: int32 [1024], replicated, may hold values from 0 to 1023, as said below
- writer_rank: int32 [1024], replicated, may hold values from 0 to 3, as said below
Outputs:
- saved: bfloat16 [3, 8, 1024, 3584], P(None, 'ep', 'dp')
Inputs may be any that keep to these rules, and one draw needn't show every extreme that they name: `expert_ids`: 8 different global expert numbers. `bucket_offsets`: each saved row named exactly once. `writer_rank`: of the bucket rows held by any one dp index, exactly 1024 // (4 * 4) are written by each dp index.
All inputs are finite; a program needn't handle non-finite values.
Results may differ from a plain program's by a relative error of at most 0.001.
Values may be sent and summed in bfloat16 or wider, within the bound.
No kernel may reach another device: no remote copies, remote signals or barrier semaphores. Data moves between devices by JAX's collectives and lax.ppermute only.
A program may use at most 128 MiB of HBM per device.

v0:
```python
import jax
import jax.numpy as jnp
from jax import lax
from jax.sharding import PartitionSpec as P


def destinations(bucket_offsets, writer_rank, shard_rows, groups):
    indicator = (writer_rank[:, None] == jnp.arange(groups, dtype=jnp.int32)[None, :]).astype(
        jnp.int32
    )
    before = jnp.cumsum(indicator, axis=0) - indicator
    within = jnp.sum(before * indicator, axis=1)
    placed = writer_rank * shard_rows + within
    return jnp.take(placed, bucket_offsets)


def route_rows(stacked, target, shard_rows, groups):
    mine = lax.axis_index("dp")
    per_pair = shard_rows // groups
    table = target.reshape(groups, shard_rows)
    outgoing = jnp.argsort(lax.dynamic_index_in_dim(table, mine, 0, keepdims=False))
    sending = jnp.take(stacked, outgoing, axis=1).reshape(3, groups, per_pair, stacked.shape[2])
    arrived = lax.all_to_all(sending, "dp", split_axis=1, concat_axis=1, tiled=True)
    ordered = jnp.sort(table, axis=1)
    slots = (
        lax.dynamic_slice_in_dim(ordered, mine * per_pair, per_pair, 1).reshape(shard_rows)
        - mine * shard_rows
    )
    return jnp.take(arrived.reshape(3, shard_rows, stacked.shape[2]), jnp.argsort(slots), axis=1)


def spread_experts(stacked, expert_ids):
    source_order = jnp.argsort(expert_ids)
    pieces = lax.all_to_all(stacked[None], "ep", split_axis=2, concat_axis=0, tiled=True)
    chosen = jnp.take(pieces, source_order, axis=0)
    return lax.all_to_all(chosen, "ep", split_axis=0, concat_axis=2, tiled=True)[0]


def on_device(master_weights, first_moment, second_moment, expert_ids, bucket_offsets, writer_rank):
    groups = lax.axis_size("dp")
    shard_rows = master_weights.shape[1]
    stacked = jnp.stack(
        [
            master_weights[0].astype(jnp.bfloat16),
            first_moment[0].astype(jnp.bfloat16),
            second_moment[0].astype(jnp.bfloat16),
        ]
    )
    target = destinations(bucket_offsets, writer_rank, shard_rows, groups)
    stacked = route_rows(stacked, target, shard_rows, groups)
    stacked = spread_experts(stacked, expert_ids)
    return stacked[:, None]


def solution(mesh):
    return jax.shard_map(
        on_device,
        mesh=mesh,
        in_specs=(P("ep", "dp", None), P("ep", "dp", None), P("ep", "dp", None), P(), P(), P()),
        out_specs=P(None, "ep", "dp", None),
        check_vma=False,
    )
```

profile of v0, /device:TPU:0, one launch (start us, length us, event | category | flops | bytes accessed | tf_op | source)
XLA Modules:
  0.0 423.0 jit_solution(14100685166902782626)
XLA Ops:
  10.3 4.5 %gather_fusion = s32[1024]{0:T(1024)S(1)} fusion(s32[1024]{0:T(1024)S(1)} %get-tuple-element.12, s32[1024]{0:T(1024)S(1)} %get-tuple-element.13), kind=kCustom, calls=%fused_computation.2 | custom fusion | bytes 12288 | tf_op jit(solution)/shard_map/jit(_take)/gather | solution.py:14
  15.5 3.2 sort.57
  18.7 2.4 convert_element_type.21
  21.1 2.8 copy.27
  24.1 2.8 copy.26
  29.2 2.8 copy.25
  32.1 14.1 %pad_maximum_fusion = bf16[3,256,3584]{2,0,1:T(4,128)(2,1)} fusion(bf16[1,256,3584]{2,0,1:T(2,128)(2,1)S(1)} %copy.27, bf16[1,256,3584]{2,0,1:T(2,128)(2,1)S(1)} %copy.26, bf16[1,256,3584]{2,0,1:T(2,128)(2,1)S(1)} %copy.25), kind=kLoop, calls=%fused_computation.4 | loop fusion | flops 16515072 | bytes 11010048 | tf_op jit(solution)/shard_map/stack | solution.py:42
  46.2 16.5 %gather_fusion.2 = bf16[256,3,3584]{2,1,0:T(4,128)(2,1)} fusion(bf16[3,256,3584]{2,0,1:T(4,128)(2,1)} %pad_maximum_fusion, s32[1024]{0:T(1024)S(1)} %pad_clamp_fusion.2), kind=kCustom, calls=%fused_computation.clone | custom fusion | bytes 11011072 | tf_op jit(solution)/shard_map/jit(_take)/gather | solution.py:22
  62.7 9.6 %broadcast_select_fusion = bf16[256,3,3584]{2,1,0:T(4,128)(2,1)} fusion(bf16[256,3,3584]{2,1,0:T(4,128)(2,1)} %gather_fusion.2, pred[256]{0:T(512)(128)(4,1)S(1)} %compare_and_fusion.1), kind=kLoop, calls=%fused_computation.6 | loop fusion | flops 2752512 | bytes 11010304 | tf_op jit(solution)/shard_map/jit(_take)/select_n | solution.py:22
  72.2 6.8 %copy.28 = bf16[3,4,64,3584]{3,2,0,1:T(8,128)(2,1)} copy(bf16[3,4,64,3584]{3,0,2,1:T(4,128)(2,1)} %bitcast.43) | data formatting | bytes 11010048 | tf_op jit(solution)/shard_map/reshape | solution.py:22
  79.1 6.3 %all-to-all-start = ((bf16[3,4,64,3584]{3,2,0,1:T(8,128)(2,1)}), bf16[3,4,64,3584]{3,2,0,1:T(8,128)(2,1)}, u32[]{:S(2)}, u32[]{:S(2)}) async-start(bf16[3,4,64,3584]{3,2,0,1:T(8,128)(2,1)} %copy.28), calls=%async_computation | async-start | bytes 11010048 | tf_op jit(solution)/shard_map/all_to_all | solution.py:23
  86.1 5.0 %sort.61.cloned.1.call-done = s32[4,256]{1,0:T(4,128)} async-done(((s32[4,256]{1,0:T(4,128)}), s32[4,256]{1,0:T(4,128)}) %sort.61.cloned.1.call-update) | async-done | bytes 4112 | tf_op jit(solution)/shard_map/jit(sort)/sort | solution.py:24
  92.0 3.2 sort.59
  95.2 112.2 %all-to-all-done = bf16[3,4,64,3584]{3,2,0,1:T(8,128)(2,1)} async-done(((bf16[3,4,64,3584]{3,2,0,1:T(8,128)(2,1)}), bf16[3,4,64,3584]{3,2,0,1:T(8,128)(2,1)}, u32[]{:S(2)}, u32[]{:S(2)}) %all-to-all-start) | async-done | bytes 5505056 | tf_op jit(solution)/shard_map/all_to_all | solution.py:23
  207.4 10.2 %copy.29 = bf16[3,4,64,3584]{3,0,2,1:T(4,128)(2,1)} copy(bf16[3,4,64,3584]{3,2,0,1:T(8,128)(2,1)} %all-to-all-done) | data formatting | bytes 11010048 | tf_op jit(solution)/shard_map/all_to_all | solution.py:23
  217.6 16.5 %gather_fusion.3 = bf16[256,3,3584]{2,1,0:T(4,128)(2,1)} fusion(bf16[3,256,3584]{2,0,1:T(4,128)(2,1)} %bitcast.44, s32[1024]{0:T(1024)S(1)} %pad_clamp_fusion.1), kind=kCustom, calls=%fused_computation.1.clone | custom fusion | bytes 11011072 | tf_op jit(solution)/shard_map/jit(_take)/gather | solution.py:29
  234.1 9.6 %select_bitcast_fusion = bf16[1,3,256,3584]{3,1,0,2:T(4,128)(2,1)} fusion(bf16[256,3,3584]{2,1,0:T(4,128)(2,1)} %gather_fusion.3, pred[256]{0:T(512)(128)(4,1)S(1)} %compare_and_fusion), kind=kLoop, calls=%fused_computation.5 | loop fusion | flops 2752512 | bytes 11010304 | tf_op jit(solution)/shard_map/broadcast_in_dim | solution.py:34
  243.7 5.0 %all-to-all-start.1 = ((bf16[1,3,256,3584]{3,1,0,2:T(4,128)(2,1)}), bf16[1,3,256,3584]{3,1,0,2:T(4,128)(2,1)}, u32[]{:S(2)}, u32[]{:S(2)}) async-start(bf16[1,3,256,3584]{3,1,0,2:T(4,128)(2,1)} %select_bitcast_fusion), calls=%async_computation.1 | async-start | bytes 14680064 | tf_op jit(solution)/shard_map/all_to_all | solution.py:34
  249.7 81.8 %all-to-all-done.1 = bf16[1,3,256,3584]{3,1,0,2:T(4,128)(2,1)} async-done(((bf16[1,3,256,3584]{3,1,0,2:T(4,128)(2,1)}), bf16[1,3,256,3584]{3,1,0,2:T(4,128)(2,1)}, u32[]{:S(2)}, u32[]{:S(2)}) %all-to-all-start.1) | async-done | bytes 5505056 | tf_op jit(solution)/shard_map/all_to_all | solution.py:34
  331.5 6.9 %copy.40 = bf16[1,3,8,32,3584]{4,3,1,2,0:T(8,128)(2,1)} copy(bf16[1,3,8,32,3584]{4,1,3,2,0:T(4,128)(2,1)} %bitcast.9) | data formatting | bytes 11010048 | tf_op jit(solution)/shard_map/all_to_all | solution.py:34
  338.4 5.8 %gather_fusion.1 = bf16[8,3,32,3584]{3,2,1,0:T(8,128)(2,1)} fusion(bf16[8,3,32,3584]{3,2,1,0:T(8,128)(2,1)} %bitcast.45, s32[1024]{0:T(1024)S(1)} %pad_clamp_fusion), kind=kCustom, calls=%fused_computation.3 | custom fusion | bytes 11010080 | tf_op jit(solution)/shard_map/jit(_take)/gather | solution.py:35
  344.2 3.2 broadcast_select_fusion.1
  347.4 65.6 %all_to_all.38 = bf16[8,3,32,3584]{3,2,1,0:T(8,128)(2,1)S(1)} all-to-all(bf16[8,3,32,3584]{3,2,1,0:T(8,128)(2,1)S(1)} %broadcast_select_fusion.1), channel_id=1, replica_groups=mesh['ep'=8,'dp'=4] {'ep'}, dimensions={0} | all-to-all | bytes 11010048 | tf_op jit(solution)/shard_map/all_to_all | solution.py:36
  413.0 2.8 copy.33
  (35 shorter events, 9.4 us)
Async XLA Ops:
  15.5 8.4 %copy-start.1 = (s32[4,256]{1,0:T(4,128)}, s32[4,256]{1,0:T(4,128)S(1)}, u32[]{:S(2)}) copy-start(s32[4,256]{1,0:T(4,128)S(1)} %select_n.39) | copy-start | bytes 12292
  18.7 5.2 %copy-start = (f32[1,256,3584]{2,1,0:T(8,128)S(1)}, f32[1,256,3584]{2,1,0:T(8,128)}, u32[]{:S(2)}) copy-start(f32[1,256,3584]{2,1,0:T(8,128)} %param.9) | copy-start | bytes 11010052
  79.1 128.3 %all-to-all-start = ((bf16[3,4,64,3584]{3,2,0,1:T(8,128)(2,1)}), bf16[3,4,64,3584]{3,2,0,1:T(8,128)(2,1)}, u32[]{:S(2)}, u32[]{:S(2)}) async-start(bf16[3,4,64,3584]{3,2,0,1:T(8,128)(2,1)} %copy.28), calls=%async_computation | async-start | bytes 11010048 | tf_op jit(solution)/shard_map/all_to_all | solution.py:23
  85.4 5.7 %sort.61.cloned.1.call-start = ((), (), s32[]{:S(2)}) async-start(), calls=%async_computation.3 | async-start | bytes 12320 | tf_op jit(solution)/shard_map/jit(sort)/sort | solution.py:24
  243.7 5.0 %copy-start.2 = (s32[8]{0:T(128)S(1)}, s32[8]{0:T(128)}, u32[]{:S(2)}) copy-start(s32[8]{0:T(128)} %param.11) | copy-start | bytes 100
  243.7 87.8 %all-to-all-start.1 = ((bf16[1,3,256,3584]{3,1,0,2:T(4,128)(2,1)}), bf16[1,3,256,3584]{3,1,0,2:T(4,128)(2,1)}, u32[]{:S(2)}, u32[]{:S(2)}) async-start(bf16[1,3,256,3584]{3,1,0,2:T(4,128)(2,1)} %select_bitcast_fusion), calls=%async_computation.1 | async-start | bytes 14680064 | tf_op jit(solution)/shard_map/all_to_all | solution.py:34
Sparse Core Ops, SparseCore 0:
  88.5 2.3 sort.63.cloned.1.call-done
  (1 shorter events, 0.0 us)
where the time goes:
time: 431 us; the launch traced here: 423 us
  waiting for transfers between devices  194 us (45%)
  local copies, waits for them, and re-layouts  84.6 us (20%)
  blocking collectives  65.6 us (15%)
  other arithmetic  53.6 us (12%)
  between operations  13.9 us (3%)
  starting transfers between devices  11.3 us (3%)
    all_to_all x1, waiting for transfers between devices, route_rows(): lax.all_to_all(sending, 'dp', split_axis=1, concat_axis=1, tiled=True)  112 us
    all_to_all x1, waiting for transfers between devices, spread_experts(): lax.all_to_all(stacked[None], 'ep', split_axis=2, concat_axis=0, tiled=True)  81.8 us
    all_to_all x1, blocking collectives, spread_experts(): lax.all_to_all(chosen, 'ep', split_axis=0, concat_axis=2, tiled=True)[0]  65.6 us
    gather x1, local copies, waits for them, and re-layouts, route_rows(): jnp.take(stacked, outgoing, axis=1)  16.5 us
    gather x1, local copies, waits for them, and re-layouts, route_rows(): jnp.take(arrived.reshape(3, shard_rows, stacked.shape[2]), jnp.argsort(sl...  16.5 us
    another operation x1, other arithmetic, on_device(): jnp.stack([master_weights[0].astype(jnp.bfloat16), first_moment[0].astype...  14.1 us
    all_to_all x1, local copies, waits for them, and re-layouts, route_rows(): lax.all_to_all(sending, 'dp', split_axis=1, concat_axis=1, tiled=True)  10.2 us
    select_n x2, other arithmetic, route_rows(): jnp.take(stacked, outgoing, axis=1)  9.58 us
  transfers between devices with their start and end apart: 2, of which 2 were waited for; matrix products, arithmetic and copies ran while one was open for 1% of the time, Pallas kernels for 0%

commit v1 on v0

v1 whole, which is shorter than its diff:
```python
import functools

import jax
import jax.numpy as jnp
from jax import lax
from jax.experimental import pallas as pl
from jax.experimental.pallas import tpu as pltpu
from jax.sharding import PartitionSpec as P


FIELDS = 3
LANES = 128
ROOM = 24 * 2**20
HBM = pl.BlockSpec(memory_space=pltpu.HBM)
SMEM = pl.BlockSpec(memory_space=pltpu.SMEM)
VMEM = pl.BlockSpec(memory_space=pltpu.VMEM)
NT = (((1,), (1,)), ((), ()))


def iota(shape, dim):
    return lax.broadcasted_iota(jnp.int32, shape, dim)


def ones_where(mask):
    return jnp.where(mask, 1.0, 0.0).astype(jnp.bfloat16)


def dot(a, b):
    return jnp.dot(a, b, preferred_element_type=jnp.float32)


def plan_kernel(groups, dp_ref, offsets_ref, writer_ref, *rest):
    send_ref, place_ref = rest[-2:]
    rows = offsets_ref.shape[1]
    shard = rows // groups
    pair = shard // groups
    me = dp_ref[0]
    writer = writer_ref[...]
    named = ones_where(offsets_ref[...] == iota((rows, rows), 0))
    holder = (iota((8, rows), 1) // shard).astype(jnp.float32).astype(jnp.bfloat16)
    source = lax.dot_general(holder, named, NT, preferred_element_type=jnp.float32)
    source = source[:1].astype(jnp.int32)
    kinds = iota((groups * groups, rows), 0)
    member = kinds == writer * groups + source
    earlier = ones_where(iota((rows, rows), 0) < iota((rows, rows), 1))
    before = dot(ones_where(member), earlier)
    count = jnp.sum(jnp.where(member, before, 0.0), axis=0, keepdims=True).astype(jnp.int32)
    within = jnp.sum(
        jnp.where(kinds // groups == writer, before, 0.0), axis=0, keepdims=True
    ).astype(jnp.int32)
    spots = iota((shard, rows), 0)
    mine = offsets_ref[:, pl.ds(pl.multiple_of(me * shard, LANES), shard)]
    leaving = ones_where((writer * pair + count == spots) & (source == me))
    send = dot(leaving, ones_where(mine == iota((rows, shard), 0)))
    send_ref[...] = send.astype(jnp.bfloat16)
    slots = ones_where((within == spots) & (writer == me))
    arrivals = ones_where(source * pair + count == spots)
    place = lax.dot_general(slots, arrivals, NT, preferred_element_type=jnp.float32)
    place_ref[...] = place.astype(jnp.bfloat16)


def copy(src, dst, sem):
    return pltpu.make_async_copy(src, dst, sem)


def split_kernel(count, start, ep_ref, w_ref, m_ref, v_ref, *rest):
    outs, (held, sem) = rest[-count - 2 : -2], rest[-2:]
    height, width = outs[0].shape[1:]
    me = ep_ref[0]
    copies = {}
    order = list(range(1, count)) + [0]
    for k in order:
        at = pl.multiple_of((me ^ k) * height, height)
        for f, ref in enumerate((w_ref, m_ref, v_ref)):
            source = ref.at[0, pl.ds(at, height), pl.ds(start, width)]
            copies[k, f] = copy(source, held.at[k, f], sem.at[k, f])
            copies[k, f].start()
    for k in order:
        for f in range(FIELDS):
            copies[k, f].wait()
            outs[k][f] = held[k, f].astype(jnp.bfloat16)


def deal(me, pieces, ordered, outs):
    height = outs[0].shape[1]
    for k in range(pieces):
        at = pl.multiple_of((me ^ k) * height, height)
        for f in range(FIELDS):
            outs[k][f] = ordered[f, pl.ds(at, height)]


def join(at_ref, ins, held):
    height = ins[0].shape[1]
    for k, ref in enumerate(ins):
        at = pl.multiple_of(at_ref[k] * height, height)
        for f in range(FIELDS):
            held[f, pl.ds(at, height)] = ref[f]


def sort_kernel(count, start, groups, dp_ref, send_ref, w_ref, m_ref, v_ref, *rest):
    outs, (held, ordered, sem) = rest[-count - 3 : -3], rest[-3:]
    width = outs[0].shape[2]
    ins = [
        copy(ref.at[0, :, pl.ds(start, width)], held.at[f], sem.at[f])
        for f, ref in enumerate((w_ref, m_ref, v_ref))
    ]
    for one in ins:
        one.start()
    for f in range(FIELDS):
        ins[f].wait()
        ordered[f] = dot(send_ref[...], held[f].astype(jnp.bfloat16)).astype(jnp.bfloat16)
    deal(dp_ref[0] * (count // groups), count, ordered, outs)


def pick_kernel(count, pick_ref, *rest):
    ins, outs = rest[:count], rest[-count:]
    for k in range(count):
        chosen = pick_ref[k]
        for j in range(count):

            @pl.when(chosen == j)
            def _():
                outs[k][...] = ins[j][...]


def route_kernel(count, groups, at_ref, dp_ref, send_ref, *rest):
    ins, outs = rest[:count], rest[-groups - 2 : -2]
    held, ordered = rest[-2:]
    join(at_ref, ins, held)
    for f in range(FIELDS):
        ordered[f] = dot(send_ref[...], held[f]).astype(jnp.bfloat16)
    deal(dp_ref[0], groups, ordered, outs)


def final_kernel(count, start, at_ref, place_ref, *rest):
    ins = rest[:count]
    saved, held, ordered, sem = rest[-4:]
    width = ins[0].shape[2]
    join(at_ref, ins, held)
    out = []
    for f in range(FIELDS):
        ordered[f] = dot(place_ref[...], held[f]).astype(jnp.bfloat16)
        one = copy(ordered.at[f], saved.at[f, 0, :, pl.ds(start, width)], sem.at[f])
        one.start()
        out.append(one)
    for one in out:
        one.wait()


def swap(piece, axis, size, shift):
    return lax.ppermute(piece, axis, [(i, i ^ shift) for i in range(size)])


def spread(pieces, ep):
    return [pieces[0]] + [swap(pieces[k], "ep", ep, k) for k in range(1, ep)]


def bf16(*shape):
    return jax.ShapeDtypeStruct(shape, jnp.bfloat16)


def on_device(ep, dp, chunks, *args):
    return exchange(ep, dp, chunks, *args)


def exchange(ep, dp, chunks, w, m, v, expert_ids, bucket_offsets, writer_rank):
    _, shard, cols = w.shape
    rows = bucket_offsets.shape[0]
    part = shard // ep
    block = shard // dp
    halves = ep // dp
    e = lax.axis_index("ep").astype(jnp.int32)
    d = lax.axis_index("dp").astype(jnp.int32)
    e1, d1 = e[None], d[None]

    numbers = jnp.arange(ep, dtype=jnp.int32)
    rank = jnp.sum((expert_ids[None, :] < expert_ids[:, None]).astype(jnp.int32), axis=1)
    target = numbers ^ e
    pick = jnp.sum(jnp.where(rank[None, :] == target[:, None], numbers[None, :], 0), axis=1) ^ e
    part_at = target
    block_at = jnp.arange(dp, dtype=jnp.int32) ^ d
    piece_at = pick[0] ^ numbers ^ (halves * d)

    def sems(*shape):
        return pltpu.SemaphoreType.DMA(shape)

    def room(width, dtype=jnp.bfloat16):
        return pltpu.VMEM((FIELDS, shard, width), dtype)

    last = []

    def call(kernel, outs, scratch, specs, args, out_space=pltpu.VMEM, **options):
        specs = specs + [pl.BlockSpec(memory_space=out_space)] * len(last)
        args = [
            one if spec is SMEM else pltpu.with_memory_space_constraint(one, spec.memory_space)
            for spec, one in zip(specs, (*args, *last))
        ]
        results = pl.pallas_call(
            kernel,
            out_shape=jax.tree.map(lambda one: out_space(one.shape, one.dtype), outs),
            in_specs=specs,
            out_specs=jax.tree.map(lambda _: pl.BlockSpec(memory_space=out_space), outs),
            scratch_shapes=scratch,
            compiler_params=pltpu.CompilerParams(vmem_limit_bytes=ROOM),
            **options,
        )(*args)
        last[:] = jax.tree.leaves(results)[-1:]
        return results

    def plan():
        return call(
            functools.partial(plan_kernel, dp),
            (bf16(shard, shard), bf16(shard, shard)),
            [],
            [SMEM, VMEM, VMEM],
            (d1, bucket_offsets.reshape(1, rows), writer_rank.reshape(1, rows)),
        )

    def split(start, width):
        return call(
            functools.partial(split_kernel, ep, start),
            (bf16(FIELDS, part, width),) * ep,
            [pltpu.VMEM((ep, FIELDS, part, width), jnp.float32), sems(ep, FIELDS)],
            [SMEM, HBM, HBM, HBM],
            (e1, w, m, v),
        )

    def sort(start, width):
        return call(
            functools.partial(sort_kernel, ep, start, dp),
            (bf16(FIELDS, part, width),) * ep,
            [room(width, jnp.float32), room(width), sems(FIELDS)],
            [SMEM, VMEM, HBM, HBM, HBM],
            (d1, send, w, m, v),
        )

    def choose(pieces):
        return call(
            functools.partial(pick_kernel, ep),
            (bf16(*pieces[0].shape),) * ep,
            [],
            [SMEM] + [VMEM] * ep,
            (pick, *pieces),
        )

    def route(pieces):
        width = pieces[0].shape[2]
        return call(
            functools.partial(route_kernel, ep, dp),
            (bf16(FIELDS, block, width),) * dp,
            [room(width), room(width)],
            [SMEM, SMEM, VMEM] + [VMEM] * ep,
            (part_at, d1, send, *pieces),
        )

    def finish(at, pieces, start):
        width = pieces[0].shape[2]
        count = len(pieces)
        last[:] = saved
        saved[:] = [
            call(
                functools.partial(final_kernel, count, start),
                bf16(FIELDS, 1, shard, cols),
                [room(width), room(width), sems(FIELDS)],
                [SMEM, VMEM] + [VMEM] * count,
                (at, place, *pieces),
                pltpu.HBM,
                **({"input_output_aliases": {2 + count: 0}} if saved else {}),
            )
        ]

    def across(pieces, step):
        far = {}
        for shift in list(range(2, dp)) + [1]:
            for k in range(shift * step, shift * step + step):
                far[k] = swap(pieces[k], "dp", dp, shift)
        return [far.get(k, piece) for k, piece in enumerate(pieces)]

    saved = []
    (c, cw), (g, gw) = [(a, n) for k, a, n in chunks if k == "ep"]
    (a, aw), (b, bw) = [(a, n) for k, a, n in chunks if k == "dp"]

    c_parts = split(c, cw)
    c_parts = spread(c_parts, ep)
    send, place = plan()
    a_parts = sort(a, aw)
    a_parts = across(a_parts, halves)
    g_parts = split(g, gw)
    g_parts = spread(g_parts, ep)
    c_parts = choose(c_parts)
    c_parts = spread(c_parts, ep)
    b_parts = sort(b, bw)
    b_parts = across(b_parts, halves)
    g_parts = choose(g_parts)
    g_parts = spread(g_parts, ep)
    c_parts = route(c_parts)
    c_parts = across(c_parts, 1)
    a_parts = spread(a_parts, ep)
    g_parts = route(g_parts)
    g_parts = across(g_parts, 1)
    b_parts = spread(b_parts, ep)
    a_parts = choose(a_parts)
    a_parts = spread(a_parts, ep)
    b_parts = choose(b_parts)
    b_parts = spread(b_parts, ep)
    finish(block_at, c_parts, c)
    finish(piece_at, a_parts, a)
    finish(piece_at, b_parts, b)
    finish(block_at, g_parts, g)
    return saved[0]


def plain_destinations(bucket_offsets, writer_rank, shard_rows, groups):
    indicator = (writer_rank[:, None] == jnp.arange(groups, dtype=jnp.int32)[None, :]).astype(jnp.int32)
    before = jnp.cumsum(indicator, axis=0) - indicator
    within = jnp.sum(before * indicator, axis=1)
    return jnp.take(writer_rank * shard_rows + within, bucket_offsets)


def plain_route(stacked, target, shard_rows, groups):
    mine = lax.axis_index("dp")
    per_pair = shard_rows // groups
    table = target.reshape(groups, shard_rows)
    outgoing = jnp.argsort(lax.dynamic_index_in_dim(table, mine, 0, keepdims=False))
    sending = jnp.take(stacked, outgoing, axis=1).reshape(FIELDS, groups, per_pair, stacked.shape[2])
    arrived = lax.all_to_all(sending, "dp", split_axis=1, concat_axis=1, tiled=True)
    ordered = jnp.sort(table, axis=1)
    slots = lax.dynamic_slice_in_dim(ordered, mine * per_pair, per_pair, 1).reshape(shard_rows)
    slots = slots - mine * shard_rows
    return jnp.take(arrived.reshape(FIELDS, shard_rows, stacked.shape[2]), jnp.argsort(slots), axis=1)


def plain_on_device(w, m, v, expert_ids, bucket_offsets, writer_rank):
    groups = lax.axis_size("dp")
    shard_rows = w.shape[1]
    stacked = jnp.stack([one[0].astype(jnp.bfloat16) for one in (w, m, v)])
    target = plain_destinations(bucket_offsets, writer_rank, shard_rows, groups)
    stacked = plain_route(stacked, target, shard_rows, groups)
    pieces = lax.all_to_all(stacked[None], "ep", split_axis=2, concat_axis=0, tiled=True)
    chosen = jnp.take(pieces, jnp.argsort(expert_ids), axis=0)
    return lax.all_to_all(chosen, "ep", split_axis=0, concat_axis=2, tiled=True)[0][:, None]


def solution(mesh):
    ep, dp = mesh.shape["ep"], mesh.shape["dp"]
    specs = dict(
        mesh=mesh,
        in_specs=(P("ep", "dp", None), P("ep", "dp", None), P("ep", "dp", None), P(), P(), P()),
        out_specs=P(None, "ep", "dp", None),
        check_vma=False,
    )

    def fits(rows, cols):
        shard = rows // dp
        return (
            ep & (ep - 1) == 0
            and dp & (dp - 1) == 0
            and ep % dp == 0
            and shard % LANES == 0
            and shard % (16 * ep) == 0
            and cols % (4 * LANES) == 0
        )

    def function(w, m, v, expert_ids, bucket_offsets, writer_rank):
        rows, cols = w.shape[1:]
        args = (w, m, v, expert_ids, bucket_offsets, writer_rank)
        if not fits(rows, cols):
            return jax.shard_map(plain_on_device, **specs)(*args)
        kinds = ("ep", "ep", "dp", "dp")
        tiles = cols // LANES
        edges = [LANES * (tiles * i // len(kinds)) for i in range(len(kinds) + 1)]
        chunks = tuple((kind, edges[i], edges[i + 1] - edges[i]) for i, kind in enumerate(kinds))
        body = jax.shard_map(functools.partial(on_device, ep, dp, chunks), **specs)
        return body(*args)

    return function
```

time: 431 us -> 255 us (0.59)
  starting transfers between devices: 11.3 us -> 94.6 us
  local copies, waits for them, and re-layouts: 84.6 us -> 8.13 us
  waiting for transfers between devices: 194 us -> 121 us
  blocking collectives: 65.6 us -> 0 us
  other arithmetic: 53.6 us -> 0.41 us
  Pallas kernels: 0 us -> 26.9 us
  between operations: 13.9 us -> 0.6 us
    all_to_all x2 -> x0, waiting for transfers between devices: 194 us -> none  [the longest x1 112 us: route_rows(): lax.all_to_all(sending, 'dp', split_axis=1, concat_axis=1, tiled=True)]
    ppermute x0 -> x74, waiting for transfers between devices: none -> 121 us  [swap(): return lax.ppermute(piece, axis, [(i, i ^ shift) for i in range(size)])]
    ppermute x0 -> x74, starting transfers between devices: none -> 94.6 us  [swap(): return lax.ppermute(piece, axis, [(i, i ^ shift) for i in range(size)])]
    all_to_all x1 -> x0, blocking collectives: 65.6 us -> none  [spread_experts(): lax.all_to_all(chosen, 'ep', split_axis=0, concat_axis=2, tiled=True)[0]]
    gather x4 -> x0, local copies, waits for them, and re-layouts: 43.3 us -> none  [the longest x1 16.5 us: route_rows(): jnp.take(stacked, outgoing, axis=1)]
    pallas_call x0 -> x15, Pallas kernels: none -> 26.9 us  [call(): pl.pallas_call(kernel, out_shape=jax.tree.map(lambda one: out_space(one.s...]
    all_to_all x3 -> x0, local copies, waits for them, and re-layouts: 20 us -> none  [the longest x1 10.2 us: route_rows(): lax.all_to_all(sending, 'dp', split_axis=1, concat_axis=1, tiled=True)]
    another operation x3 -> x0, other arithmetic: 15.4 us -> none  [the longest x1 14.1 us: on_device(): jnp.stack([master_weights[0].astype(jnp.bfloat16), first_moment[0].astype...]
  transfers between devices with their start and end apart: 2 -> 74, of which waited for: 2 -> 22; matrix products, arithmetic and copies ran while one was open for 1% -> 0% of each run, Pallas kernels for 0% -> 9%
where the time goes in v1:
time: 255 us; the launch traced here: 251 us
  waiting for transfers between devices  121 us (47%)
  starting transfers between devices  94.6 us (37%)
  Pallas kernels  26.9 us (11%)
  local copies, waits for them, and re-layouts  8.13 us (3%)
    ppermute x74, waiting for transfers between devices, swap(): return lax.ppermute(piece, axis, [(i, i ^ shift) for i in range(size)])  121 us
    ppermute x74, starting transfers between devices, swap(): return lax.ppermute(piece, axis, [(i, i ^ shift) for i in range(size)])  94.6 us
    pallas_call x15, Pallas kernels, call(): pl.pallas_call(kernel, out_shape=jax.tree.map(lambda one: out_space(one.s...  26.9 us
    unnamed x62, local copies, waits for them, and re-layouts  8.13 us
  transfers between devices with their start and end apart: 74, of which 22 were waited for; matrix products, arithmetic and copies ran while one was open for 0% of the time, Pallas kernels for 9%

profile of v1, /device:TPU:0, one launch (start us, length us, event | category | flops | bytes accessed | tf_op | source)
XLA Modules:
  0.0 251.1 jit_solution(8969856121945939685)
XLA Ops:
  2.6 2.6 %collective-permute-start.8 = (bf16[3,32,896]{2,1,0:T(8,128)(2,1)S(1)}, bf16[3,32,896]{2,1,0:T(8,128)(2,1)S(1)}, u32[]{:S(2)}, u32[]{:S(2)}) collective-permute-start(bf16[3,32,896]{2,1,0:T(8,128)(2,1)S(1)} %get-tuple-element.93), channel_id=1, source_target_pairs={{0,8},{4,12},{8,0},{12,4},{16,24},{20,28},{24,16},{28,20},{1,9},{5... | collective-permute-start | bytes 516104 | tf_op jit(solution)/shard_map/ppermute | solution.py:151
  7.0 2.6 %collective-permute-start.12 = (bf16[3,32,896]{2,1,0:T(8,128)(2,1)S(1)}, bf16[3,32,896]{2,1,0:T(8,128)(2,1)S(1)}, u32[]{:S(2)}, u32[]{:S(2)}) collective-permute-start(bf16[3,32,896]{2,1,0:T(8,128)(2,1)S(1)} %get-tuple-element.97), channel_id=1, source_target_pairs={{0,24},{4,28},{8,16},{12,20},{16,8},{20,12},{24,0},{28,4},{1,25},{... | collective-permute-start | bytes 516104 | tf_op jit(solution)/shard_map/ppermute | solution.py:151
  18.9 3.3 %collective-permute-done.11.rest_5_ = bf16[3,32,896]{2,1,0:T(8,128)(2,1)S(1)} collective-permute-done((bf16[3,32,896]{2,1,0:T(8,128)(2,1)S(1)}, bf16[3,32,896]{2,1,0:T(8,128)(2,1)S(1)}, u32[]{:S(2)}, u32[]{:S(2)}) %collective-permute-start.11) | collective-permute-done | bytes 172064 | tf_op jit(solution)/shard_map/ppermute | solution.py:151
  24.1 2.6 %collective-permute-start.49 = (bf16[3,32,896]{2,1,0:T(8,128)(2,1)S(1)}, bf16[3,32,896]{2,1,0:T(8,128)(2,1)S(1)}, u32[]{:S(2)}, u32[]{:S(2)}) collective-permute-start(bf16[3,32,896]{2,1,0:T(8,128)(2,1)S(1)} %get-tuple-element.131), channel_id=1, source_target_pairs={{0,2},{1,3},{2,0},{3,1},{4,6},{5,7},{6,4},{7,5},{8,10},{9,11},{10,... | collective-permute-start | bytes 516104 | tf_op jit(solution)/shard_map/ppermute | solution.py:151
  27.1 2.5 collective-permute-start.53
  33.0 14.0 %collective-permute-done.49 = bf16[3,32,896]{2,1,0:T(8,128)(2,1)S(1)} collective-permute-done((bf16[3,32,896]{2,1,0:T(8,128)(2,1)S(1)}, bf16[3,32,896]{2,1,0:T(8,128)(2,1)S(1)}, u32[]{:S(2)}, u32[]{:S(2)}) %collective-permute-start.49) | collective-permute-done | bytes 172064 | tf_op jit(solution)/shard_map/ppermute | solution.py:151
  58.2 8.0 %collective-permute-start.48 = (bf16[3,32,896]{2,1,0:T(8,128)(2,1)S(1)}, bf16[3,32,896]{2,1,0:T(8,128)(2,1)S(1)}, u32[]{:S(2)}, u32[]{:S(2)}) collective-permute-start(bf16[3,32,896]{2,1,0:T(8,128)(2,1)S(1)} %collective-permute-done.47), channel_id=1, source_target_pairs={{0,12},{4,8},{8,4},{12,0},{16,28},{20,24},{24,20},{28,16},{1,13},{... | collective-permute-start | bytes 516104 | tf_op jit(solution)/shard_map/ppermute | solution.py:151
  66.2 3.1 %collective-permute-done.4.rest_5_ = bf16[3,32,896]{2,1,0:T(8,128)(2,1)S(1)} collective-permute-done((bf16[3,32,896]{2,1,0:T(8,128)(2,1)S(1)}, bf16[3,32,896]{2,1,0:T(8,128)(2,1)S(1)}, u32[]{:S(2)}, u32[]{:S(2)}) %collective-permute-start.4) | collective-permute-done | bytes 172064 | tf_op jit(solution)/shard_map/ppermute | solution.py:151
  75.0 8.7 %collective-permute-done.50.rest_4_ = bf16[3,32,896]{2,1,0:T(8,128)(2,1)S(1)} collective-permute-done((bf16[3,32,896]{2,1,0:T(8,128)(2,1)S(1)}, bf16[3,32,896]{2,1,0:T(8,128)(2,1)S(1)}, u32[]{:S(2)}, u32[]{:S(2)}) %collective-permute-start.50) | collective-permute-done | bytes 172064 | tf_op jit(solution)/shard_map/ppermute | solution.py:151
  95.6 8.4 %collective-permute-done.25.rest_5_ = bf16[3,32,896]{2,1,0:T(8,128)(2,1)S(1)} collective-permute-done((bf16[3,32,896]{2,1,0:T(8,128)(2,1)S(1)}, bf16[3,32,896]{2,1,0:T(8,128)(2,1)S(1)}, u32[]{:S(2)}, u32[]{:S(2)}) %collective-permute-start.25) | collective-permute-done | bytes 172064 | tf_op jit(solution)/shard_map/ppermute | solution.py:151
  111.0 8.4 %collective-permute-done.17.rest_4_ = bf16[3,32,896]{2,1,0:T(8,128)(2,1)S(1)} collective-permute-done((bf16[3,32,896]{2,1,0:T(8,128)(2,1)S(1)}, bf16[3,32,896]{2,1,0:T(8,128)(2,1)S(1)}, u32[]{:S(2)}, u32[]{:S(2)}) %collective-permute-start.17) | collective-permute-done | bytes 172064 | tf_op jit(solution)/shard_map/ppermute | solution.py:151
  119.5 2.9 %collective-permute-start.32 = (bf16[3,32,896]{2,1,0:T(8,128)(2,1)S(1)}, bf16[3,32,896]{2,1,0:T(8,128)(2,1)S(1)}, u32[]{:S(2)}, u32[]{:S(2)}) collective-permute-start(bf16[3,32,896]{2,1,0:T(8,128)(2,1)S(1)} %get-tuple-element.122), channel_id=1, source_target_pairs={{0,1},{1,0},{2,3},{3,2},{4,5},{5,4},{6,7},{7,6},{8,9},{9,8},{10,11... | collective-permute-start | bytes 516104 | tf_op jit(solution)/shard_map/ppermute | solution.py:151
  126.9 2.5 collective-permute-start.40
  136.2 10.7 %collective-permute-done.36 = bf16[3,32,896]{2,1,0:T(8,128)(2,1)S(1)} collective-permute-done((bf16[3,32,896]{2,1,0:T(8,128)(2,1)S(1)}, bf16[3,32,896]{2,1,0:T(8,128)(2,1)S(1)}, u32[]{:S(2)}, u32[]{:S(2)}) %collective-permute-start.36) | collective-permute-done | bytes 172064 | tf_op jit(solution)/shard_map/ppermute | solution.py:151
  146.9 3.7 %collective-permute-done.38 = bf16[3,32,896]{2,1,0:T(8,128)(2,1)S(1)} collective-permute-done((bf16[3,32,896]{2,1,0:T(8,128)(2,1)S(1)}, bf16[3,32,896]{2,1,0:T(8,128)(2,1)S(1)}, u32[]{:S(2)}, u32[]{:S(2)}) %collective-permute-start.38) | collective-permute-done | bytes 172064 | tf_op jit(solution)/shard_map/ppermute | solution.py:151
  155.1 2.7 %collective-permute-done.33.rest_2_ = bf16[3,32,896]{2,1,0:T(8,128)(2,1)S(1)} collective-permute-done((bf16[3,32,896]{2,1,0:T(8,128)(2,1)S(1)}, bf16[3,32,896]{2,1,0:T(8,128)(2,1)S(1)}, u32[]{:S(2)}, u32[]{:S(2)}) %collective-permute-start.33) | collective-permute-done | bytes 172064 | tf_op jit(solution)/shard_map/ppermute | solution.py:151
  162.8 7.3 %collective-permute-done.39.rest_5_ = bf16[3,32,896]{2,1,0:T(8,128)(2,1)S(1)} collective-permute-done((bf16[3,32,896]{2,1,0:T(8,128)(2,1)S(1)}, bf16[3,32,896]{2,1,0:T(8,128)(2,1)S(1)}, u32[]{:S(2)}, u32[]{:S(2)}) %collective-permute-start.39) | collective-permute-done | bytes 172064 | tf_op jit(solution)/shard_map/ppermute | solution.py:151
  178.0 6.4 %collective-permute-done.68.rest_5_ = bf16[3,32,896]{2,1,0:T(8,128)(2,1)S(1)} collective-permute-done((bf16[3,32,896]{2,1,0:T(8,128)(2,1)S(1)}, bf16[3,32,896]{2,1,0:T(8,128)(2,1)S(1)}, u32[]{:S(2)}, u32[]{:S(2)}) %collective-permute-start.68) | collective-permute-done | bytes 172064 | tf_op jit(solution)/shard_map/ppermute | solution.py:151
  186.0 5.9 %collective-permute-start.71 = (bf16[3,64,896]{2,1,0:T(8,128)(2,1)S(1)}, bf16[3,64,896]{2,1,0:T(8,128)(2,1)S(1)}, u32[]{:S(2)}, u32[]{:S(2)}) collective-permute-start(bf16[3,64,896]{2,1,0:T(8,128)(2,1)S(1)} %get-tuple-element.151), channel_id=1, source_target_pairs={{0,1},{1,0},{2,3},{3,2},{4,5},{5,4},{6,7},{7,6},{8,9},{9,8},{10,11... | collective-permute-start | bytes 1032200 | tf_op jit(solution)/shard_map/ppermute | solution.py:151
  197.9 5.6 %collective-permute-done.60.rest_4_ = bf16[3,32,896]{2,1,0:T(8,128)(2,1)S(1)} collective-permute-done((bf16[3,32,896]{2,1,0:T(8,128)(2,1)S(1)}, bf16[3,32,896]{2,1,0:T(8,128)(2,1)S(1)}, u32[]{:S(2)}, u32[]{:S(2)}) %collective-permute-start.60) | collective-permute-done | bytes 172064 | tf_op jit(solution)/shard_map/ppermute | solution.py:151
  205.3 2.5 collective-permute-start.29
  209.3 10.1 %collective-permute-done.72.rest_2_ = bf16[3,64,896]{2,1,0:T(8,128)(2,1)S(1)} collective-permute-done((bf16[3,64,896]{2,1,0:T(8,128)(2,1)}, bf16[3,64,896]{2,1,0:T(8,128)(2,1)S(1)}, u32[]{:S(2)}, u32[]{:S(2)}) %collective-permute-start.72) | collective-permute-done | bytes 344096 | tf_op jit(solution)/shard_map/ppermute | solution.py:151
  220.4 2.5 shard_map.75.rest_8_
  230.2 18.7 %collective-permute-done.29.rest_2_ = bf16[3,64,896]{2,1,0:T(8,128)(2,1)S(1)} collective-permute-done((bf16[3,64,896]{2,1,0:T(8,128)(2,1)}, bf16[3,64,896]{2,1,0:T(8,128)(2,1)S(1)}, u32[]{:S(2)}, u32[]{:S(2)}) %collective-permute-start.29) | collective-permute-done | bytes 344096 | tf_op jit(solution)/shard_map/ppermute | solution.py:151
  (207 shorter events, 104.8 us)
Async XLA Ops:
  7.0 17.1 %collective-permute-start.12 = (bf16[3,32,896]{2,1,0:T(8,128)(2,1)S(1)}, bf16[3,32,896]{2,1,0:T(8,128)(2,1)S(1)}, u32[]{:S(2)}, u32[]{:S(2)}) collective-permute-start(bf16[3,32,896]{2,1,0:T(8,128)(2,1)S(1)} %get-tuple-element.97), channel_id=1, source_target_pairs={{0,24},{4,28},{8,16},{12,20},{16,8},{20,12},{24,0},{28,4},{1,25},{... | collective-permute-start | bytes 516104 | tf_op jit(solution)/shard_map/ppermute | solution.py:151
  24.1 22.9 %collective-permute-start.49 = (bf16[3,32,896]{2,1,0:T(8,128)(2,1)S(1)}, bf16[3,32,896]{2,1,0:T(8,128)(2,1)S(1)}, u32[]{:S(2)}, u32[]{:S(2)}) collective-permute-start(bf16[3,32,896]{2,1,0:T(8,128)(2,1)S(1)} %get-tuple-element.131), channel_id=1, source_target_pairs={{0,2},{1,3},{2,0},{3,1},{4,6},{5,7},{6,4},{7,5},{8,10},{9,11},{10,... | collective-permute-start | bytes 516104 | tf_op jit(solution)/shard_map/ppermute | solution.py:151
  26.7 24.0 %collective-permute-start.51 = (bf16[3,32,896]{2,1,0:T(8,128)(2,1)S(1)}, bf16[3,32,896]{2,1,0:T(8,128)(2,1)S(1)}, u32[]{:S(2)}, u32[]{:S(2)}) collective-permute-start(bf16[3,32,896]{2,1,0:T(8,128)(2,1)S(1)} %get-tuple-element.132), channel_id=1, source_target_pairs={{0,2},{1,3},{2,0},{3,1},{4,6},{5,7},{6,4},{7,5},{8,10},{9,11},{10,... | collective-permute-start | bytes 516104 | tf_op jit(solution)/shard_map/ppermute | solution.py:151
  27.1 23.9 %collective-permute-start.53 = (bf16[3,32,896]{2,1,0:T(8,128)(2,1)S(1)}, bf16[3,32,896]{2,1,0:T(8,128)(2,1)S(1)}, u32[]{:S(2)}, u32[]{:S(2)}) collective-permute-start(bf16[3,32,896]{2,1,0:T(8,128)(2,1)S(1)} %get-tuple-element.133), channel_id=1, source_target_pairs={{0,3},{1,2},{2,1},{3,0},{4,7},{5,6},{6,5},{7,4},{8,11},{9,10},{10,... | collective-permute-start | bytes 516104 | tf_op jit(solution)/shard_map/ppermute | solution.py:151
  31.6 20.9 %collective-permute-start.55 = (bf16[3,32,896]{2,1,0:T(8,128)(2,1)S(1)}, bf16[3,32,896]{2,1,0:T(8,128)(2,1)S(1)}, u32[]{:S(2)}, u32[]{:S(2)}) collective-permute-start(bf16[3,32,896]{2,1,0:T(8,128)(2,1)S(1)} %get-tuple-element.82.rest_0_), channel_id=1, source_target_pairs={{0,3},{1,2},{2,1},{3,0},{4,7},{5,6},{6,5},{7,4},{8,11},{9,10},{10,... | collective-permute-start | bytes 516104 | tf_op jit(solution)/shard_map/ppermute | solution.py:151
  33.0 21.0 %collective-permute-start = (bf16[3,32,896]{2,1,0:T(8,128)(2,1)S(1)}, bf16[3,32,896]{2,1,0:T(8,128)(2,1)S(1)}, u32[]{:S(2)}, u32[]{:S(2)}) collective-permute-start(bf16[3,32,896]{2,1,0:T(8,128)(2,1)S(1)} %get-tuple-element.84), channel_id=1, source_target_pairs={{0,4},{4,0},{8,12},{12,8},{16,20},{20,16},{24,28},{28,24},{1,5},{5... | collective-permute-start | bytes 516104 | tf_op jit(solution)/shard_map/ppermute | solution.py:151
  52.5 16.8 %collective-permute-start.4 = (bf16[3,32,896]{2,1,0:T(8,128)(2,1)S(1)}, bf16[3,32,896]{2,1,0:T(8,128)(2,1)S(1)}, u32[]{:S(2)}, u32[]{:S(2)}) collective-permute-start(bf16[3,32,896]{2,1,0:T(8,128)(2,1)S(1)} %get-tuple-element.88), channel_id=1, source_target_pairs={{0,20},{4,16},{8,28},{12,24},{16,4},{20,0},{24,12},{28,8},{1,21},{... | collective-permute-start | bytes 516104 | tf_op jit(solution)/shard_map/ppermute | solution.py:151
  54.0 16.9 %collective-permute-start.5 = (bf16[3,32,896]{2,1,0:T(8,128)(2,1)S(1)}, bf16[3,32,896]{2,1,0:T(8,128)(2,1)S(1)}, u32[]{:S(2)}, u32[]{:S(2)}) collective-permute-start(bf16[3,32,896]{2,1,0:T(8,128)(2,1)S(1)} %get-tuple-element.89), channel_id=1, source_target_pairs={{0,24},{4,28},{8,16},{12,20},{16,8},{20,12},{24,0},{28,4},{1,25},{... | collective-permute-start | bytes 516104 | tf_op jit(solution)/shard_map/ppermute | solution.py:151
  106.4 17.6 %collective-permute-start.19 = (bf16[3,32,896]{2,1,0:T(8,128)(2,1)S(1)}, bf16[3,32,896]{2,1,0:T(8,128)(2,1)S(1)}, u32[]{:S(2)}, u32[]{:S(2)}) collective-permute-start(bf16[3,32,896]{2,1,0:T(8,128)(2,1)S(1)} %get-tuple-element.106), channel_id=1, source_target_pairs={{0,24},{4,28},{8,16},{12,20},{16,8},{20,12},{24,0},{28,4},{1,25},{... | collective-permute-start | bytes 516104 | tf_op jit(solution)/shard_map/ppermute | solution.py:151
  108.5 16.9 %collective-permute-start.20 = (bf16[3,32,896]{2,1,0:T(8,128)(2,1)S(1)}, bf16[3,32,896]{2,1,0:T(8,128)(2,1)S(1)}, u32[]{:S(2)}, u32[]{:S(2)}) collective-permute-start(bf16[3,32,896]{2,1,0:T(8,128)(2,1)S(1)} %get-tuple-element.107.rest_8_), channel_id=1, source_target_pairs={{0,28},{4,24},{8,20},{12,16},{16,12},{20,8},{24,4},{28,0},{1,29},{... | collective-permute-start | bytes 516104 | tf_op jit(solution)/shard_map/ppermute | solution.py:151
  109.6 17.3 %collective-permute-start.31 = (bf16[3,32,896]{2,1,0:T(8,128)(2,1)S(1)}, bf16[3,32,896]{2,1,0:T(8,128)(2,1)S(1)}, u32[]{:S(2)}, u32[]{:S(2)}) collective-permute-start(bf16[3,32,896]{2,1,0:T(8,128)(2,1)S(1)} %get-tuple-element.121), channel_id=1, source_target_pairs={{0,4},{4,0},{8,12},{12,8},{16,20},{20,16},{24,28},{28,24},{1,5},{5... | collective-permute-start | bytes 516104 | tf_op jit(solution)/shard_map/ppermute | solution.py:151
  124.0 22.9 %collective-permute-start.36 = (bf16[3,32,896]{2,1,0:T(8,128)(2,1)S(1)}, bf16[3,32,896]{2,1,0:T(8,128)(2,1)S(1)}, u32[]{:S(2)}, u32[]{:S(2)}) collective-permute-start(bf16[3,32,896]{2,1,0:T(8,128)(2,1)S(1)} %get-tuple-element.124), channel_id=1, source_target_pairs={{0,2},{1,3},{2,0},{3,1},{4,6},{5,7},{6,4},{7,5},{8,10},{9,11},{10,... | collective-permute-start | bytes 516104 | tf_op jit(solution)/shard_map/ppermute | solution.py:151
  125.4 25.1 %collective-permute-start.38 = (bf16[3,32,896]{2,1,0:T(8,128)(2,1)S(1)}, bf16[3,32,896]{2,1,0:T(8,128)(2,1)S(1)}, u32[]{:S(2)}, u32[]{:S(2)}) collective-permute-start(bf16[3,32,896]{2,1,0:T(8,128)(2,1)S(1)} %get-tuple-element.125), channel_id=1, source_target_pairs={{0,2},{1,3},{2,0},{3,1},{4,6},{5,7},{6,4},{7,5},{8,10},{9,11},{10,... | collective-permute-start | bytes 516104 | tf_op jit(solution)/shard_map/ppermute | solution.py:151
  126.9 23.9 %collective-permute-start.40 = (bf16[3,32,896]{2,1,0:T(8,128)(2,1)S(1)}, bf16[3,32,896]{2,1,0:T(8,128)(2,1)S(1)}, u32[]{:S(2)}, u32[]{:S(2)}) collective-permute-start(bf16[3,32,896]{2,1,0:T(8,128)(2,1)S(1)} %get-tuple-element.126), channel_id=1, source_target_pairs={{0,3},{1,2},{2,1},{3,0},{4,7},{5,6},{6,5},{7,4},{8,11},{9,10},{10,... | collective-permute-start | bytes 516104 | tf_op jit(solution)/shard_map/ppermute | solution.py:151
  152.2 17.8 %collective-permute-start.39 = (bf16[3,32,896]{2,1,0:T(8,128)(2,1)S(1)}, bf16[3,32,896]{2,1,0:T(8,128)(2,1)S(1)}, u32[]{:S(2)}, u32[]{:S(2)}) collective-permute-start(bf16[3,32,896]{2,1,0:T(8,128)(2,1)S(1)} %collective-permute-done.38), channel_id=1, source_target_pairs={{0,20},{4,16},{8,28},{12,24},{16,4},{20,0},{24,12},{28,8},{1,21},{... | collective-permute-start | bytes 516104 | tf_op jit(solution)/shard_map/ppermute | solution.py:151
  172.2 19.7 %collective-permute-start.70 = (bf16[3,32,896]{2,1,0:T(8,128)(2,1)S(1)}, bf16[3,32,896]{2,1,0:T(8,128)(2,1)S(1)}, u32[]{:S(2)}, u32[]{:S(2)}) collective-permute-start(bf16[3,32,896]{2,1,0:T(8,128)(2,1)S(1)} %get-tuple-element.134.rest_8_), channel_id=1, source_target_pairs={{0,28},{4,24},{8,20},{12,16},{16,12},{20,8},{24,4},{28,0},{1,29},{... | collective-permute-start | bytes 516104 | tf_op jit(solution)/shard_map/ppermute | solution.py:151
  176.0 17.6 %collective-permute-start.57 = (bf16[3,32,896]{2,1,0:T(8,128)(2,1)S(1)}, bf16[3,32,896]{2,1,0:T(8,128)(2,1)S(1)}, u32[]{:S(2)}, u32[]{:S(2)}) collective-permute-start(bf16[3,32,896]{2,1,0:T(8,128)(2,1)S(1)} %get-tuple-element.136), channel_id=1, source_target_pairs={{0,4},{4,0},{8,12},{12,8},{16,20},{20,16},{24,28},{28,24},{1,5},{5... | collective-permute-start | bytes 516104 | tf_op jit(solution)/shard_map/ppermute | solution.py:151
  176.8 18.9 %collective-permute-start.58 = (bf16[3,32,896]{2,1,0:T(8,128)(2,1)S(1)}, bf16[3,32,896]{2,1,0:T(8,128)(2,1)S(1)}, u32[]{:S(2)}, u32[]{:S(2)}) collective-permute-start(bf16[3,32,896]{2,1,0:T(8,128)(2,1)S(1)} %get-tuple-element.137), channel_id=1, source_target_pairs={{0,8},{4,12},{8,0},{12,4},{16,24},{20,28},{24,16},{28,20},{1,9},{5... | collective-permute-start | bytes 516104 | tf_op jit(solution)/shard_map/ppermute | solution.py:151
  186.0 21.8 %collective-permute-start.71 = (bf16[3,64,896]{2,1,0:T(8,128)(2,1)S(1)}, bf16[3,64,896]{2,1,0:T(8,128)(2,1)S(1)}, u32[]{:S(2)}, u32[]{:S(2)}) collective-permute-start(bf16[3,64,896]{2,1,0:T(8,128)(2,1)S(1)} %get-tuple-element.151), channel_id=1, source_target_pairs={{0,1},{1,0},{2,3},{3,2},{4,5},{5,4},{6,7},{7,6},{8,9},{9,8},{10,11... | collective-permute-start | bytes 1032200 | tf_op jit(solution)/shard_map/ppermute | solution.py:151
  192.6 26.8 %collective-permute-start.72 = (bf16[3,64,896]{2,1,0:T(8,128)(2,1)}, bf16[3,64,896]{2,1,0:T(8,128)(2,1)S(1)}, u32[]{:S(2)}, u32[]{:S(2)}) collective-permute-start(bf16[3,64,896]{2,1,0:T(8,128)(2,1)} %get-tuple-element.152), channel_id=1, source_target_pairs={{0,2},{1,3},{2,0},{3,1},{4,6},{5,7},{6,4},{7,5},{8,10},{9,11},{10,... | collective-permute-start | bytes 1032200 | tf_op jit(solution)/shard_map/ppermute | solution.py:151
  194.3 26.1 %collective-permute-start.73 = (bf16[3,64,896]{2,1,0:T(8,128)(2,1)S(1)}, bf16[3,64,896]{2,1,0:T(8,128)(2,1)}, u32[]{:S(2)}, u32[]{:S(2)}) collective-permute-start(bf16[3,64,896]{2,1,0:T(8,128)(2,1)S(1)} %get-tuple-element.115.rest_8_), channel_id=1, source_target_pairs={{0,3},{1,2},{2,1},{3,0},{4,7},{5,6},{6,5},{7,4},{8,11},{9,10},{10,... | collective-permute-start | bytes 1032200 | tf_op jit(solution)/shard_map/ppermute | solution.py:151
  204.2 26.0 %collective-permute-start.28 = (bf16[3,64,896]{2,1,0:T(8,128)(2,1)}, bf16[3,64,896]{2,1,0:T(8,128)(2,1)S(1)}, u32[]{:S(2)}, u32[]{:S(2)}) collective-permute-start(bf16[3,64,896]{2,1,0:T(8,128)(2,1)} %get-tuple-element.117), channel_id=1, source_target_pairs={{0,1},{1,0},{2,3},{3,2},{4,5},{5,4},{6,7},{7,6},{8,9},{9,8},{10,11... | collective-permute-start | bytes 1032200 | tf_op jit(solution)/shard_map/ppermute | solution.py:151
  205.3 43.6 %collective-permute-start.29 = (bf16[3,64,896]{2,1,0:T(8,128)(2,1)}, bf16[3,64,896]{2,1,0:T(8,128)(2,1)S(1)}, u32[]{:S(2)}, u32[]{:S(2)}) collective-permute-start(bf16[3,64,896]{2,1,0:T(8,128)(2,1)} %get-tuple-element.118), channel_id=1, source_target_pairs={{0,2},{1,3},{2,0},{3,1},{4,6},{5,7},{6,4},{7,5},{8,10},{9,11},{10,... | collective-permute-start | bytes 1032200 | tf_op jit(solution)/shard_map/ppermute | solution.py:151
  207.8 41.1 %collective-permute-start.30 = (bf16[3,64,896]{2,1,0:T(8,128)(2,1)S(1)}, bf16[3,64,896]{2,1,0:T(8,128)(2,1)S(1)}, u32[]{:S(2)}, u32[]{:S(2)}) collective-permute-start(bf16[3,64,896]{2,1,0:T(8,128)(2,1)S(1)} %get-tuple-element.119.rest_8_), channel_id=1, source_target_pairs={{0,3},{1,2},{2,1},{3,0},{4,7},{5,6},{6,5},{7,4},{8,11},{9,10},{10,... | collective-permute-start | bytes 1032200 | tf_op jit(solution)/shard_map/ppermute | solution.py:151
  (81 other events, 884.5 us)

commit v2 on v1

--- a/solution.py
+++ b/solution.py
@@ -11,6 +11,7 @@
 FIELDS = 3
 LANES = 128
 ROOM = 24 * 2**20
+SHARES = (9, 5, 9, 5)
 HBM = pl.BlockSpec(memory_space=pltpu.HBM)
 SMEM = pl.BlockSpec(memory_space=pltpu.SMEM)
 VMEM = pl.BlockSpec(memory_space=pltpu.VMEM)
@@ -29,32 +30,38 @@
     return jnp.dot(a, b, preferred_element_type=jnp.float32)
 
 
-def plan_kernel(groups, dp_ref, offsets_ref, writer_ref, *rest):
-    send_ref, place_ref = rest[-2:]
+def plan(groups, dp_ref, offsets_ref, writer_ref, send_ref, place_ref):
     rows = offsets_ref.shape[1]
     shard = rows // groups
     pair = shard // groups
     me = dp_ref[0]
     writer = writer_ref[...]
-    named = ones_where(offsets_ref[...] == iota((rows, rows), 0))
-    holder = (iota((8, rows), 1) // shard).astype(jnp.float32).astype(jnp.bfloat16)
-    source = lax.dot_general(holder, named, NT, preferred_element_type=jnp.float32)
-    source = source[:1].astype(jnp.int32)
+    offsets = offsets_ref[...]
+    high = jnp.where(offsets // LANES == iota((rows // LANES, rows), 0), iota((1, rows), 1) // shard, 0)
+    low = ones_where(offsets % LANES == iota((LANES, rows), 0))
+    high = high.astype(jnp.float32).astype(jnp.bfloat16)
+    source = lax.dot_general(high, low, NT, preferred_element_type=jnp.float32).astype(jnp.int32)
+    source = jnp.concatenate([source[i : i + 1] for i in range(rows // LANES)], axis=1)
     kinds = iota((groups * groups, rows), 0)
-    member = kinds == writer * groups + source
-    earlier = ones_where(iota((rows, rows), 0) < iota((rows, rows), 1))
-    before = dot(ones_where(member), earlier)
-    count = jnp.sum(jnp.where(member, before, 0.0), axis=0, keepdims=True).astype(jnp.int32)
+    member = jnp.where(kinds == writer * groups + source, 1.0, 0.0)
+    earlier = ones_where(iota((LANES, LANES), 0) < iota((LANES, LANES), 1))
+    before, total = [], jnp.zeros((groups * groups, 1), jnp.float32)
+    for i in range(rows // LANES):
+        some = member[:, i * LANES : (i + 1) * LANES]
+        before.append(dot(some.astype(jnp.bfloat16), earlier) + total)
+        total = total + jnp.sum(some, axis=1, keepdims=True)
+    before = jnp.concatenate(before, axis=1)
+    count = jnp.sum(member * before, axis=0, keepdims=True).astype(jnp.int32)
     within = jnp.sum(
         jnp.where(kinds // groups == writer, before, 0.0), axis=0, keepdims=True
     ).astype(jnp.int32)
     spots = iota((shard, rows), 0)
     mine = offsets_ref[:, pl.ds(pl.multiple_of(me * shard, LANES), shard)]
-    leaving = ones_where((writer * pair + count == spots) & (source == me))
+    leaving = ones_where(((writer ^ me) * pair + count == spots) & (source == me))
     send = dot(leaving, ones_where(mine == iota((rows, shard), 0)))
     send_ref[...] = send.astype(jnp.bfloat16)
     slots = ones_where((within == spots) & (writer == me))
-    arrivals = ones_where(source * pair + count == spots)
+    arrivals = ones_where((source ^ me) * pair + count == spots)
     place = lax.dot_general(slots, arrivals, NT, preferred_element_type=jnp.float32)
     place_ref[...] = place.astype(jnp.bfloat16)
 
@@ -63,30 +70,71 @@
     return pltpu.make_async_copy(src, dst, sem)
 
 
+def part_copies(start, ep_ref, refs, held, sem):
+    count, _, height, width = held.shape
+    me = ep_ref[0]
+    copies = []
+    for k in range(count):
+        at = pl.multiple_of((me ^ k) * height, height)
+        for f, ref in enumerate(refs):
+            source = ref.at[0, pl.ds(at, height), pl.ds(start, width)]
+            copies.append(copy(source, held.at[k, f], sem.at[k, f]))
+    for one in copies:
+        one.start()
+    return copies
+
+
+def round_parts(copies, held, outs):
+    for k, out in enumerate(outs):
+        for f in range(FIELDS):
+            copies[k * FIELDS + f].wait()
+            out[f] = held[k, f].astype(jnp.bfloat16)
+
+
+def row_copies(start, refs, held, sem):
+    width = held.shape[2]
+    copies = [
+        copy(ref.at[0, :, pl.ds(start, width)], held.at[f], sem.at[f]) for f, ref in enumerate(refs)
+    ]
+    for one in copies:
+        one.start()
+    return copies
+
+
+def sort_rows(copies, send_ref, held, outs):
+    for f in range(FIELDS):
+        copies[f].wait()
+        deal(dot(send_ref[...], held[f].astype(jnp.bfloat16)), f, outs)
+
+
+def first_kernel(
+    count, groups, parts_start, rows_start, ep_ref, dp_ref, offsets_ref, writer_ref, w_ref, m_ref, v_ref, *rest
+):
+    parts_out, rows_out = rest[:count], rest[count : 2 * count]
+    send_ref, place_ref, offsets, writer, parts_held, rows_held, table_sem, parts_sem, rows_sem = rest[2 * count :]
+    refs = (w_ref, m_ref, v_ref)
+    tables = [copy(offsets_ref, offsets, table_sem.at[0]), copy(writer_ref, writer, table_sem.at[1])]
+    for one in tables:
+        one.start()
+    parts = part_copies(parts_start, ep_ref, refs, parts_held, parts_sem)
+    rows = row_copies(rows_start, refs, rows_held, rows_sem)
+    for one in tables:
+        one.wait()
+    plan(groups, dp_ref, offsets, writer, send_ref, place_ref)
+    round_parts(parts, parts_held, parts_out)
+    sort_rows(rows, send_ref, rows_held, rows_out)
+
+
 def split_kernel(count, start, ep_ref, w_ref, m_ref, v_ref, *rest):
     outs, (held, sem) = rest[-count - 2 : -2], rest[-2:]
-    height, width = outs[0].shape[1:]
-    me = ep_ref[0]
-    copies = {}
-    order = list(range(1, count)) + [0]
-    for k in order:
-        at = pl.multiple_of((me ^ k) * height, height)
-        for f, ref in enumerate((w_ref, m_ref, v_ref)):
-            source = ref.at[0, pl.ds(at, height), pl.ds(start, width)]
-            copies[k, f] = copy(source, held.at[k, f], sem.at[k, f])
-            copies[k, f].start()
-    for k in order:
-        for f in range(FIELDS):
-            copies[k, f].wait()
-            outs[k][f] = held[k, f].astype(jnp.bfloat16)
-
-
-def deal(me, pieces, ordered, outs):
+    copies = part_copies(start, ep_ref, (w_ref, m_ref, v_ref), held, sem)
+    round_parts(copies, held, outs)
+
+
+def deal(rows, f, outs):
     height = outs[0].shape[1]
-    for k in range(pieces):
-        at = pl.multiple_of((me ^ k) * height, height)
-        for f in range(FIELDS):
-            outs[k][f] = ordered[f, pl.ds(at, height)]
+    for k, out in enumerate(outs):
+        out[f] = rows[k * height : (k + 1) * height].astype(jnp.bfloat16)
 
 
 def join(at_ref, ins, held):
@@ -97,19 +145,9 @@
             held[f, pl.ds(at, height)] = ref[f]
 
 
-def sort_kernel(count, start, groups, dp_ref, send_ref, w_ref, m_ref, v_ref, *rest):
-    outs, (held, ordered, sem) = rest[-count - 3 : -3], rest[-3:]
-    width = outs[0].shape[2]
-    ins = [
-        copy(ref.at[0, :, pl.ds(start, width)], held.at[f], sem.at[f])
-        for f, ref in enumerate((w_ref, m_ref, v_ref))
-    ]
-    for one in ins:
-        one.start()
-    for f in range(FIELDS):
-        ins[f].wait()
-        ordered[f] = dot(send_ref[...], held[f].astype(jnp.bfloat16)).astype(jnp.bfloat16)
-    deal(dp_ref[0] * (count // groups), count, ordered, outs)
+def sort_kernel(count, start, send_ref, w_ref, m_ref, v_ref, *rest):
+    outs, (held, sem) = rest[-count - 2 : -2], rest[-2:]
+    sort_rows(row_copies(start, (w_ref, m_ref, v_ref), held, sem), send_ref, held, outs)
 
 
 def pick_kernel(count, pick_ref, *rest):
@@ -123,26 +161,28 @@
                 outs[k][...] = ins[j][...]
 
 
-def route_kernel(count, groups, at_ref, dp_ref, send_ref, *rest):
-    ins, outs = rest[:count], rest[-groups - 2 : -2]
-    held, ordered = rest[-2:]
+def route_kernel(count, groups, at_ref, send_ref, *rest):
+    ins, outs, held = rest[:count], rest[-groups - 1 : -1], rest[-1]
     join(at_ref, ins, held)
     for f in range(FIELDS):
-        ordered[f] = dot(send_ref[...], held[f]).astype(jnp.bfloat16)
-    deal(dp_ref[0], groups, ordered, outs)
-
-
-def final_kernel(count, start, at_ref, place_ref, *rest):
-    ins = rest[:count]
-    saved, held, ordered, sem = rest[-4:]
-    width = ins[0].shape[2]
-    join(at_ref, ins, held)
+        deal(dot(send_ref[...], held[f]), f, outs)
+
+
+def final_kernel(counts, starts, place_ref, *rest):
+    chunks = len(counts)
+    ats, rest = rest[:chunks], rest[chunks:]
+    saved, scratch, sem = rest[-2 * chunks - 2], rest[-2 * chunks - 1 : -1], rest[-1]
     out = []
-    for f in range(FIELDS):
-        ordered[f] = dot(place_ref[...], held[f]).astype(jnp.bfloat16)
-        one = copy(ordered.at[f], saved.at[f, 0, :, pl.ds(start, width)], sem.at[f])
-        one.start()
-        out.append(one)
+    for i, count in enumerate(counts):
+        ins, rest = rest[:count], rest[count:]
+        held, ordered = scratch[2 * i], scratch[2 * i + 1]
+        width = held.shape[2]
+        join(ats[i], ins, held)
+        for f in range(FIELDS):
+            ordered[f] = dot(place_ref[...], held[f]).astype(jnp.bfloat16)
+            one = copy(ordered.at[f], saved.at[f, 0, :, pl.ds(starts[i], width)], sem.at[i, f])
+            one.start()
+            out.append(one)
     for one in out:
         one.wait()
 
@@ -151,8 +191,17 @@
     return lax.ppermute(piece, axis, [(i, i ^ shift) for i in range(size)])
 
 
+def far_first(size):
+    return list(range(2, size)) + [1]
+
+
+def wide_order(ep):
+    return sorted(range(2, ep), key=lambda k: ((k // 2).bit_count() > 1, k % 2, k)) + [1]
+
+
 def spread(pieces, ep):
-    return [pieces[0]] + [swap(pieces[k], "ep", ep, k) for k in range(1, ep)]
+    far = {k: swap(pieces[k], "ep", ep, k) for k in wide_order(ep)}
+    return [far.get(k, piece) for k, piece in enumerate(pieces)]
 
 
 def bf16(*shape):
@@ -178,8 +227,8 @@
     target = numbers ^ e
     pick = jnp.sum(jnp.where(rank[None, :] == target[:, None], numbers[None, :], 0), axis=1) ^ e
     part_at = target
-    block_at = jnp.arange(dp, dtype=jnp.int32) ^ d
-    piece_at = pick[0] ^ numbers ^ (halves * d)
+    block_at = jnp.arange(dp, dtype=jnp.int32)
+    piece_at = pick[0] ^ numbers
 
     def sems(*shape):
         return pltpu.SemaphoreType.DMA(shape)
@@ -207,14 +256,24 @@
         last[:] = jax.tree.leaves(results)[-1:]
         return results
 
-    def plan():
-        return call(
-            functools.partial(plan_kernel, dp),
-            (bf16(shard, shard), bf16(shard, shard)),
-            [],
-            [SMEM, VMEM, VMEM],
-            (d1, bucket_offsets.reshape(1, rows), writer_rank.reshape(1, rows)),
-        )
+    def first(c, cw, a, aw):
+        pieces = (ep, FIELDS, part, cw)
+        results = call(
+            functools.partial(first_kernel, ep, dp, c, a),
+            (bf16(FIELDS, part, cw),) * ep + (bf16(FIELDS, part, aw),) * ep + (bf16(shard, shard),) * 2,
+            [
+                pltpu.VMEM((1, rows), jnp.int32),
+                pltpu.VMEM((1, rows), jnp.int32),
+                pltpu.VMEM(pieces, jnp.float32),
+                room(aw, jnp.float32),
+                sems(2),
+                sems(ep, FIELDS),
+                sems(FIELDS),
+            ],
+            [SMEM, SMEM, HBM, HBM, HBM, HBM, HBM],
+            (e1, d1, bucket_offsets.reshape(1, rows), writer_rank.reshape(1, rows), w, m, v),
+        )
+        return list(results[:ep]), list(results[ep : 2 * ep]), *results[2 * ep :]
 
     def split(start, width):
         return call(
@@ -227,11 +286,11 @@
 
     def sort(start, width):
         return call(
-            functools.partial(sort_kernel, ep, start, dp),
+            functools.partial(sort_kernel, ep, start),
             (bf16(FIELDS, part, width),) * ep,
-            [room(width, jnp.float32), room(width), sems(FIELDS)],
-            [SMEM, VMEM, HBM, HBM, HBM],
-            (d1, send, w, m, v),
+            [room(width, jnp.float32), sems(FIELDS)],
+            [VMEM, HBM, HBM, HBM],
+            (send, w, m, v),
         )
 
     def choose(pieces):
@@ -248,30 +307,31 @@
         return call(
             functools.partial(route_kernel, ep, dp),
             (bf16(FIELDS, block, width),) * dp,
-            [room(width), room(width)],
-            [SMEM, SMEM, VMEM] + [VMEM] * ep,
-            (part_at, d1, send, *pieces),
-        )
-
-    def finish(at, pieces, start):
-        width = pieces[0].shape[2]
-        count = len(pieces)
+            [room(width)],
+            [SMEM, VMEM] + [VMEM] * ep,
+            (part_at, send, *pieces),
+        )
+
+    def finish(*chunks):
+        counts = tuple(len(pieces) for _, pieces, _ in chunks)
+        widths = [pieces[0].shape[2] for _, pieces, _ in chunks]
+        total = sum(counts)
         last[:] = saved
         saved[:] = [
             call(
-                functools.partial(final_kernel, count, start),
+                functools.partial(final_kernel, counts, tuple(start for _, _, start in chunks)),
                 bf16(FIELDS, 1, shard, cols),
-                [room(width), room(width), sems(FIELDS)],
-                [SMEM, VMEM] + [VMEM] * count,
-                (at, place, *pieces),
+                [room(width) for width in widths for _ in range(2)] + [sems(len(chunks), FIELDS)],
+                [VMEM] + [SMEM] * len(chunks) + [VMEM] * total,
+                (place, *[at for at, _, _ in chunks], *[one for _, pieces, _ in chunks for one in pieces]),
                 pltpu.HBM,
-                **({"input_output_aliases": {2 + count: 0}} if saved else {}),
+                **({"input_output_aliases": {1 + len(chunks) + total: 0}} if saved else {}),
             )
         ]
 
     def across(pieces, step):
         far = {}
-        for shift in list(range(2, dp)) + [1]:
+        for shift in far_first(dp):
             for k in range(shift * step, shift * step + step):
                 far[k] = swap(pieces[k], "dp", dp, shift)
         return [far.get(k, piece) for k, piece in enumerate(pieces)]
@@ -280,10 +340,8 @@
     (c, cw), (g, gw) = [(a, n) for k, a, n in chunks if k == "ep"]
     (a, aw), (b, bw) = [(a, n) for k, a, n in chunks if k == "dp"]
 
-    c_parts = split(c, cw)
+    c_parts, a_parts, send, place = first(c, cw, a, aw)
     c_parts = spread(c_parts, ep)
-    send, place = plan()
-    a_parts = sort(a, aw)
     a_parts = across(a_parts, halves)
     g_parts = split(g, gw)
     g_parts = spread(g_parts, ep)
@@ -303,10 +361,9 @@
     a_parts = spread(a_parts, ep)
     b_parts = choose(b_parts)
     b_parts = spread(b_parts, ep)
-    finish(block_at, c_parts, c)
-    finish(piece_at, a_parts, a)
-    finish(piece_at, b_parts, b)
-    finish(block_at, g_parts, g)
+    finish((block_at, c_parts, c))
+    finish((piece_at, a_parts, a))
+    finish((piece_at, b_parts, b), (block_at, g_parts, g))
     return saved[0]
 
 
@@ -358,7 +415,9 @@
             and ep % dp == 0
             and shard % LANES == 0
             and shard % (16 * ep) == 0
-            and cols % (4 * LANES) == 0
+            and cols % LANES == 0
+            and rows % LANES == 0
+            and cols // LANES >= sum(SHARES)
         )
 
     def function(w, m, v, expert_ids, bucket_offsets, writer_rank):
@@ -368,7 +427,7 @@
             return jax.shard_map(plain_on_device, **specs)(*args)
         kinds = ("ep", "ep", "dp", "dp")
         tiles = cols // LANES
-        edges = [LANES * (tiles * i // len(kinds)) for i in range(len(kinds) + 1)]
+        edges = [LANES * (tiles * sum(SHARES[:i]) // sum(SHARES)) for i in range(len(SHARES) + 1)]
         chunks = tuple((kind, edges[i], edges[i + 1] - edges[i]) for i, kind in enumerate(kinds))
         body = jax.shard_map(functools.partial(on_device, ep, dp, chunks), **specs)
         return body(*args)

time: 255 us -> 252 us (0.988)
  local copies, waits for them, and re-layouts: 8.13 us -> 0.01 us
  starting transfers between devices: 94.6 us -> 101 us
  waiting for transfers between devices: 121 us -> 126 us
  Pallas kernels: 26.9 us -> 22.3 us
    unnamed x62 -> x2, local copies, waits for them, and re-layouts: 8.13 us -> 0.01 us
    ppermute x74, starting transfers between devices: 94.6 us -> 101 us  [swap(): return lax.ppermute(piece, axis, [(i, i ^ shift) for i in range(size)])]
    ppermute x74, waiting for transfers between devices: 121 us -> 126 us  [swap(): return lax.ppermute(piece, axis, [(i, i ^ shift) for i in range(size)])]
    pallas_call x15 -> x12, Pallas kernels: 26.9 us -> 22.3 us  [call(): pl.pallas_call(kernel, out_shape=jax.tree.map(lambda one: out_space(one.s...]
  transfers between devices with their start and end apart: 74 -> 74, of which waited for: 22 -> 27; matrix products, arithmetic and copies ran while one was open for 0% -> 0% of each run, Pallas kernels for 9% -> 5%
where the time goes in v2:
time: 252 us; the launch traced here: 250 us
  waiting for transfers between devices  126 us (50%)
  starting transfers between devices  101 us (40%)
  Pallas kernels  22.3 us (9%)
    ppermute x74, waiting for transfers between devices, swap(): return lax.ppermute(piece, axis, [(i, i ^ shift) for i in range(size)])  126 us
    ppermute x74, starting transfers between devices, swap(): return lax.ppermute(piece, axis, [(i, i ^ shift) for i in range(size)])  101 us
    pallas_call x12, Pallas kernels, call(): pl.pallas_call(kernel, out_shape=jax.tree.map(lambda one: out_space(one.s...  22.3 us
  transfers between devices with their start and end apart: 74, of which 27 were waited for; matrix products, arithmetic and copies ran while one was open for 0% of the time, Pallas kernels for 5%

profile of v2, /device:TPU:0, one launch (start us, length us, event | category | flops | bytes accessed | tf_op | source)
XLA Modules:
  0.0 250.2 jit_solution(15924933950046465361)
XLA Ops:
  0.0 5.2 %shard_map.64 = (bf16[3,32,1152]{2,1,0:T(8,128)(2,1)S(1)}, bf16[3,32,1152]{2,1,0:T(8,128)(2,1)S(1)}, bf16[3,32,1152]{2,1,0:T(8,128)(2,1)S(1)}, bf16[3,32,1152]{2...) custom-call(s32[1]{0:T(128)} %bitcast.ep_ref, ...), custom_call_target="tpu_custom_call" | custom-call | tf_op jit(solution)/shard_map/pallas_call | solution.py:247
  11.9 2.7 %collective-permute-start.38 = (bf16[3,32,640]{2,1,0:T(8,128)(2,1)S(1)}, bf16[3,32,640]{2,1,0:T(8,128)(2,1)S(1)}, u32[]{:S(2)}, u32[]{:S(2)}) collective-permute-start(bf16[3,32,640]{2,1,0:T(8,128)(2,1)S(1)} %get-tuple-element.113), channel_id=1, source_target_pairs={{0,24},{4,28},{8,16},{12,20},{16,8},{20,12},{24,0},{28,4},{1,25},{... | collective-permute-start | bytes 368648 | tf_op jit(solution)/shard_map/ppermute | solution.py:191
  23.8 9.3 %collective-permute-done.39.rest_7_ = bf16[3,32,640]{2,1,0:T(8,128)(2,1)S(1)} collective-permute-done((bf16[3,32,640]{2,1,0:T(8,128)(2,1)S(1)}, bf16[3,32,640]{2,1,0:T(8,128)(2,1)S(1)}, u32[]{:S(2)}, u32[]{:S(2)}) %collective-permute-start.39) | collective-permute-done | bytes 122912 | tf_op jit(solution)/shard_map/ppermute | solution.py:191
  38.0 12.2 %collective-permute-done.4.rest_5_ = bf16[3,32,1152]{2,1,0:T(8,128)(2,1)S(1)} collective-permute-done((bf16[3,32,1152]{2,1,0:T(8,128)(2,1)S(1)}, bf16[3,32,1152]{2,1,0:T(8,128)(2,1)S(1)}, u32[]{:S(2)}, u32[]{:S(2)}) %collective-permute-start.4) | collective-permute-done | bytes 221216 | tf_op jit(solution)/shard_map/ppermute | solution.py:191
  51.7 2.6 %collective-permute-start.25 = (bf16[3,32,1152]{2,1,0:T(8,128)(2,1)S(1)}, bf16[3,32,1152]{2,1,0:T(8,128)(2,1)S(1)}, u32[]{:S(2)}, u32[]{:S(2)}) collective-permute-start(bf16[3,32,1152]{2,1,0:T(8,128)(2,1)S(1)} %get-tuple-element.103), channel_id=1, source_target_pairs={{0,2},{1,3},{2,0},{3,1},{4,6},{5,7},{6,4},{7,5},{8,10},{9,11},{10,... | collective-permute-start | bytes 663560 | tf_op jit(solution)/shard_map/ppermute | solution.py:191
  62.5 17.4 %collective-permute-done.25 = bf16[3,32,1152]{2,1,0:T(8,128)(2,1)S(1)} collective-permute-done((bf16[3,32,1152]{2,1,0:T(8,128)(2,1)S(1)}, bf16[3,32,1152]{2,1,0:T(8,128)(2,1)S(1)}, u32[]{:S(2)}, u32[]{:S(2)}) %collective-permute-start.25) | collective-permute-done | bytes 221216 | tf_op jit(solution)/shard_map/ppermute | solution.py:191
  81.4 3.2 %collective-permute-done.27 = bf16[3,32,1152]{2,1,0:T(8,128)(2,1)S(1)} collective-permute-done((bf16[3,32,1152]{2,1,0:T(8,128)(2,1)S(1)}, bf16[3,32,1152]{2,1,0:T(8,128)(2,1)S(1)}, u32[]{:S(2)}, u32[]{:S(2)}) %collective-permute-start.27) | collective-permute-done | bytes 221216 | tf_op jit(solution)/shard_map/ppermute | solution.py:191
  90.7 6.0 %collective-permute-start.8 = (bf16[3,32,640]{2,1,0:T(8,128)(2,1)S(1)}, bf16[3,32,640]{2,1,0:T(8,128)(2,1)S(1)}, u32[]{:S(2)}, u32[]{:S(2)}) collective-permute-start(bf16[3,32,640]{2,1,0:T(8,128)(2,1)S(1)} %get-tuple-element.93), channel_id=1, source_target_pairs={{0,1},{1,0},{2,3},{3,2},{4,5},{5,4},{6,7},{7,6},{8,9},{9,8},{10,11... | collective-permute-start | bytes 368648 | tf_op jit(solution)/shard_map/ppermute | solution.py:191
  98.7 4.9 %collective-permute-start.10 = (bf16[3,32,640]{2,1,0:T(8,128)(2,1)S(1)}, bf16[3,32,640]{2,1,0:T(8,128)(2,1)S(1)}, u32[]{:S(2)}, u32[]{:S(2)}) collective-permute-start(bf16[3,32,640]{2,1,0:T(8,128)(2,1)S(1)} %get-tuple-element.94), channel_id=1, source_target_pairs={{0,1},{1,0},{2,3},{3,2},{4,5},{5,4},{6,7},{7,6},{8,9},{9,8},{10,11... | collective-permute-start | bytes 368648 | tf_op jit(solution)/shard_map/ppermute | solution.py:191
  110.6 7.0 %collective-permute-done.12 = bf16[3,32,640]{2,1,0:T(8,128)(2,1)S(1)} collective-permute-done((bf16[3,32,640]{2,1,0:T(8,128)(2,1)S(1)}, bf16[3,32,640]{2,1,0:T(8,128)(2,1)S(1)}, u32[]{:S(2)}, u32[]{:S(2)}) %collective-permute-start.12) | collective-permute-done | bytes 122912 | tf_op jit(solution)/shard_map/ppermute | solution.py:191
  122.5 4.5 %collective-permute-done.18 = bf16[3,32,640]{2,1,0:T(8,128)(2,1)S(1)} collective-permute-done((bf16[3,32,640]{2,1,0:T(8,128)(2,1)S(1)}, bf16[3,32,640]{2,1,0:T(8,128)(2,1)S(1)}, u32[]{:S(2)}, u32[]{:S(2)}) %collective-permute-start.18) | collective-permute-done | bytes 122912 | tf_op jit(solution)/shard_map/ppermute | solution.py:191
  127.0 3.2 %collective-permute-start.30 = (bf16[3,32,1152]{2,1,0:T(8,128)(2,1)S(1)}, bf16[3,32,1152]{2,1,0:T(8,128)(2,1)S(1)}, u32[]{:S(2)}, u32[]{:S(2)}) collective-permute-start(bf16[3,32,1152]{2,1,0:T(8,128)(2,1)S(1)} %collective-permute-done.29), channel_id=1, source_target_pairs={{0,24},{4,28},{8,16},{12,20},{16,8},{20,12},{24,0},{28,4},{1,25},{... | collective-permute-start | bytes 663560 | tf_op jit(solution)/shard_map/ppermute | solution.py:191
  131.3 8.8 %collective-permute-start.49 = (bf16[3,32,1152]{2,1,0:T(8,128)(2,1)S(1)}, bf16[3,32,1152]{2,1,0:T(8,128)(2,1)S(1)}, u32[]{:S(2)}, u32[]{:S(2)}) collective-permute-start(bf16[3,32,1152]{2,1,0:T(8,128)(2,1)S(1)} %get-tuple-element.125), channel_id=1, source_target_pairs={{0,12},{4,8},{8,4},{12,0},{16,28},{20,24},{24,20},{28,16},{1,13},{... | collective-permute-start | bytes 663560 | tf_op jit(solution)/shard_map/ppermute | solution.py:191
  142.7 3.8 %collective-permute-done.48.rest_2_ = bf16[3,32,1152]{2,1,0:T(8,128)(2,1)S(1)} collective-permute-done((bf16[3,32,1152]{2,1,0:T(8,128)(2,1)S(1)}, bf16[3,32,1152]{2,1,0:T(8,128)(2,1)S(1)}, u32[]{:S(2)}, u32[]{:S(2)}) %collective-permute-start.48) | collective-permute-done | bytes 221216 | tf_op jit(solution)/shard_map/ppermute | solution.py:191
  146.5 3.6 %collective-permute-done.49.rest_3_ = bf16[3,32,1152]{2,1,0:T(8,128)(2,1)S(1)} collective-permute-done((bf16[3,32,1152]{2,1,0:T(8,128)(2,1)S(1)}, bf16[3,32,1152]{2,1,0:T(8,128)(2,1)S(1)}, u32[]{:S(2)}, u32[]{:S(2)}) %collective-permute-start.49) | collective-permute-done | bytes 221216 | tf_op jit(solution)/shard_map/ppermute | solution.py:191
  150.8 7.1 %collective-permute-done.50.rest_4_ = bf16[3,32,1152]{2,1,0:T(8,128)(2,1)S(1)} collective-permute-done((bf16[3,32,1152]{2,1,0:T(8,128)(2,1)S(1)}, bf16[3,32,1152]{2,1,0:T(8,128)(2,1)S(1)}, u32[]{:S(2)}, u32[]{:S(2)}) %collective-permute-start.50) | collective-permute-done | bytes 221216 | tf_op jit(solution)/shard_map/ppermute | solution.py:191
  167.7 2.6 %collective-permute-done.13.rest_4_ = bf16[3,32,640]{2,1,0:T(8,128)(2,1)S(1)} collective-permute-done((bf16[3,32,640]{2,1,0:T(8,128)(2,1)S(1)}, bf16[3,32,640]{2,1,0:T(8,128)(2,1)S(1)}, u32[]{:S(2)}, u32[]{:S(2)}) %collective-permute-start.13) | collective-permute-done | bytes 122912 | tf_op jit(solution)/shard_map/ppermute | solution.py:191
  170.4 3.4 %collective-permute-done.15.rest_5_ = bf16[3,32,640]{2,1,0:T(8,128)(2,1)S(1)} collective-permute-done((bf16[3,32,640]{2,1,0:T(8,128)(2,1)S(1)}, bf16[3,32,640]{2,1,0:T(8,128)(2,1)S(1)}, u32[]{:S(2)}, u32[]{:S(2)}) %collective-permute-start.15) | collective-permute-done | bytes 122912 | tf_op jit(solution)/shard_map/ppermute | solution.py:191
  178.6 2.5 %collective-permute-done.55.rest_4_ = bf16[3,32,640]{2,1,0:T(8,128)(2,1)S(1)} collective-permute-done((bf16[3,32,640]{2,1,0:T(8,128)(2,1)S(1)}, bf16[3,32,640]{2,1,0:T(8,128)(2,1)S(1)}, u32[]{:S(2)}, u32[]{:S(2)}) %collective-permute-start.55) | collective-permute-done | bytes 122912 | tf_op jit(solution)/shard_map/ppermute | solution.py:191
  191.4 3.0 %collective-permute-start.73 = (bf16[3,64,1152]{2,1,0:T(8,128)(2,1)S(1)}, bf16[3,64,1152]{2,1,0:T(8,128)(2,1)S(1)}, u32[]{:S(2)}, u32[]{:S(2)}) collective-permute-start(bf16[3,64,1152]{2,1,0:T(8,128)(2,1)S(1)} %get-tuple-element.129.rest_8_), channel_id=1, source_target_pairs={{0,3},{1,2},{2,1},{3,0},{4,7},{5,6},{6,5},{7,4},{8,11},{9,10},{10,... | collective-permute-start | bytes 1327112 | tf_op jit(solution)/shard_map/ppermute | solution.py:191
  197.4 6.2 %collective-permute-done.69.rest_7_ = bf16[3,32,1152]{2,1,0:T(8,128)(2,1)S(1)} collective-permute-done((bf16[3,32,1152]{2,1,0:T(8,128)(2,1)S(1)}, bf16[3,32,1152]{2,1,0:T(8,128)(2,1)S(1)}, u32[]{:S(2)}, u32[]{:S(2)}) %collective-permute-start.69) | collective-permute-done | bytes 221216 | tf_op jit(solution)/shard_map/ppermute | solution.py:191
  206.0 3.5 %collective-permute-start.62 = (bf16[3,64,640]{2,1,0:T(8,128)(2,1)S(1)}, bf16[3,64,640]{2,1,0:T(8,128)(2,1)S(1)}, u32[]{:S(2)}, u32[]{:S(2)}) collective-permute-start(bf16[3,64,640]{2,1,0:T(8,128)(2,1)S(1)} %get-tuple-element.142), channel_id=1, source_target_pairs={{0,2},{1,3},{2,0},{3,1},{4,6},{5,7},{6,4},{7,5},{8,10},{9,11},{10,... | collective-permute-start | bytes 737288 | tf_op jit(solution)/shard_map/ppermute | solution.py:191
  209.7 12.7 %collective-permute-done.72.rest_3_ = bf16[3,64,1152]{2,1,0:T(8,128)(2,1)S(1)} collective-permute-done((bf16[3,64,1152]{2,1,0:T(8,128)(2,1)S(1)}, bf16[3,64,1152]{2,1,0:T(8,128)(2,1)S(1)}, u32[]{:S(2)}, u32[]{:S(2)}) %collective-permute-start.72) | collective-permute-done | bytes 442400 | tf_op jit(solution)/shard_map/ppermute | solution.py:191
  230.5 17.2 %collective-permute-done.62.rest_12_ = bf16[3,64,640]{2,1,0:T(8,128)(2,1)S(1)} collective-permute-done((bf16[3,64,640]{2,1,0:T(8,128)(2,1)S(1)}, bf16[3,64,640]{2,1,0:T(8,128)(2,1)S(1)}, u32[]{:S(2)}, u32[]{:S(2)}) %collective-permute-start.62) | collective-permute-done | bytes 245792 | tf_op jit(solution)/shard_map/ppermute | solution.py:191
  (145 shorter events, 97.4 us)
Async XLA Ops:
  14.6 18.5 %collective-permute-start = (bf16[3,32,1152]{2,1,0:T(8,128)(2,1)S(1)}, bf16[3,32,1152]{2,1,0:T(8,128)(2,1)S(1)}, u32[]{:S(2)}, u32[]{:S(2)}) collective-permute-start(bf16[3,32,1152]{2,1,0:T(8,128)(2,1)S(1)} %get-tuple-element.82), channel_id=1, source_target_pairs={{0,4},{4,0},{8,12},{12,8},{16,20},{20,16},{24,28},{28,24},{1,5},{5... | collective-permute-start | bytes 663560 | tf_op jit(solution)/shard_map/ppermute | solution.py:191
  16.5 19.0 %collective-permute-start.1 = (bf16[3,32,1152]{2,1,0:T(8,128)(2,1)S(1)}, bf16[3,32,1152]{2,1,0:T(8,128)(2,1)S(1)}, u32[]{:S(2)}, u32[]{:S(2)}) collective-permute-start(bf16[3,32,1152]{2,1,0:T(8,128)(2,1)S(1)} %get-tuple-element.83), channel_id=1, source_target_pairs={{0,8},{4,12},{8,0},{12,4},{16,24},{20,28},{24,16},{28,20},{1,9},{5... | collective-permute-start | bytes 663560 | tf_op jit(solution)/shard_map/ppermute | solution.py:191
  17.9 17.9 %collective-permute-start.2 = (bf16[3,32,1152]{2,1,0:T(8,128)(2,1)S(1)}, bf16[3,32,1152]{2,1,0:T(8,128)(2,1)S(1)}, u32[]{:S(2)}, u32[]{:S(2)}) collective-permute-start(bf16[3,32,1152]{2,1,0:T(8,128)(2,1)S(1)} %get-tuple-element.84), channel_id=1, source_target_pairs={{0,12},{4,8},{8,4},{12,0},{16,28},{20,24},{24,20},{28,16},{1,13},{... | collective-permute-start | bytes 663560 | tf_op jit(solution)/shard_map/ppermute | solution.py:191
  33.1 18.6 %collective-permute-start.5 = (bf16[3,32,1152]{2,1,0:T(8,128)(2,1)S(1)}, bf16[3,32,1152]{2,1,0:T(8,128)(2,1)S(1)}, u32[]{:S(2)}, u32[]{:S(2)}) collective-permute-start(bf16[3,32,1152]{2,1,0:T(8,128)(2,1)S(1)} %get-tuple-element.87), channel_id=1, source_target_pairs={{0,24},{4,28},{8,16},{12,20},{16,8},{20,12},{24,0},{28,4},{1,25},{... | collective-permute-start | bytes 663560 | tf_op jit(solution)/shard_map/ppermute | solution.py:191
  35.5 18.8 %collective-permute-start.6 = (bf16[3,32,1152]{2,1,0:T(8,128)(2,1)S(1)}, bf16[3,32,1152]{2,1,0:T(8,128)(2,1)S(1)}, u32[]{:S(2)}, u32[]{:S(2)}) collective-permute-start(bf16[3,32,1152]{2,1,0:T(8,128)(2,1)S(1)} %get-tuple-element.88), channel_id=1, source_target_pairs={{0,28},{4,24},{8,20},{12,16},{16,12},{20,8},{24,4},{28,0},{1,29},{... | collective-permute-start | bytes 663560 | tf_op jit(solution)/shard_map/ppermute | solution.py:191
  35.8 18.9 %collective-permute-start.20 = (bf16[3,32,1152]{2,1,0:T(8,128)(2,1)S(1)}, bf16[3,32,1152]{2,1,0:T(8,128)(2,1)S(1)}, u32[]{:S(2)}, u32[]{:S(2)}) collective-permute-start(bf16[3,32,1152]{2,1,0:T(8,128)(2,1)S(1)} %get-tuple-element.100), channel_id=1, source_target_pairs={{0,4},{4,0},{8,12},{12,8},{16,20},{20,16},{24,28},{28,24},{1,5},{5... | collective-permute-start | bytes 663560 | tf_op jit(solution)/shard_map/ppermute | solution.py:191
  36.2 21.0 %collective-permute-start.21 = (bf16[3,32,1152]{2,1,0:T(8,128)(2,1)S(1)}, bf16[3,32,1152]{2,1,0:T(8,128)(2,1)S(1)}, u32[]{:S(2)}, u32[]{:S(2)}) collective-permute-start(bf16[3,32,1152]{2,1,0:T(8,128)(2,1)S(1)} %get-tuple-element.101), channel_id=1, source_target_pairs={{0,1},{1,0},{2,3},{3,2},{4,5},{5,4},{6,7},{7,6},{8,9},{9,8},{10,11... | collective-permute-start | bytes 663560 | tf_op jit(solution)/shard_map/ppermute | solution.py:191
  51.7 28.2 %collective-permute-start.25 = (bf16[3,32,1152]{2,1,0:T(8,128)(2,1)S(1)}, bf16[3,32,1152]{2,1,0:T(8,128)(2,1)S(1)}, u32[]{:S(2)}, u32[]{:S(2)}) collective-permute-start(bf16[3,32,1152]{2,1,0:T(8,128)(2,1)S(1)} %get-tuple-element.103), channel_id=1, source_target_pairs={{0,2},{1,3},{2,0},{3,1},{4,6},{5,7},{6,4},{7,5},{8,10},{9,11},{10,... | collective-permute-start | bytes 663560 | tf_op jit(solution)/shard_map/ppermute | solution.py:191
  54.3 30.3 %collective-permute-start.27 = (bf16[3,32,1152]{2,1,0:T(8,128)(2,1)S(1)}, bf16[3,32,1152]{2,1,0:T(8,128)(2,1)S(1)}, u32[]{:S(2)}, u32[]{:S(2)}) collective-permute-start(bf16[3,32,1152]{2,1,0:T(8,128)(2,1)S(1)} %get-tuple-element.104), channel_id=1, source_target_pairs={{0,2},{1,3},{2,0},{3,1},{4,6},{5,7},{6,4},{7,5},{8,10},{9,11},{10,... | collective-permute-start | bytes 663560 | tf_op jit(solution)/shard_map/ppermute | solution.py:191
  54.7 30.0 %collective-permute-start.29 = (bf16[3,32,1152]{2,1,0:T(8,128)(2,1)S(1)}, bf16[3,32,1152]{2,1,0:T(8,128)(2,1)S(1)}, u32[]{:S(2)}, u32[]{:S(2)}) collective-permute-start(bf16[3,32,1152]{2,1,0:T(8,128)(2,1)S(1)} %get-tuple-element.105), channel_id=1, source_target_pairs={{0,3},{1,2},{2,1},{3,0},{4,7},{5,6},{6,5},{7,4},{8,11},{9,10},{10,... | collective-permute-start | bytes 663560 | tf_op jit(solution)/shard_map/ppermute | solution.py:191
  57.1 28.0 %collective-permute-start.31 = (bf16[3,32,1152]{2,1,0:T(8,128)(2,1)S(1)}, bf16[3,32,1152]{2,1,0:T(8,128)(2,1)S(1)}, u32[]{:S(2)}, u32[]{:S(2)}) collective-permute-start(bf16[3,32,1152]{2,1,0:T(8,128)(2,1)S(1)} %get-tuple-element.106), channel_id=1, source_target_pairs={{0,3},{1,2},{2,1},{3,0},{4,7},{5,6},{6,5},{7,4},{8,11},{9,10},{10,... | collective-permute-start | bytes 663560 | tf_op jit(solution)/shard_map/ppermute | solution.py:191
  62.4 25.2 %collective-permute-start.40 = (bf16[3,32,640]{2,1,0:T(8,128)(2,1)S(1)}, bf16[3,32,640]{2,1,0:T(8,128)(2,1)S(1)}, u32[]{:S(2)}, u32[]{:S(2)}) collective-permute-start(bf16[3,32,640]{2,1,0:T(8,128)(2,1)S(1)} %get-tuple-element.115), channel_id=1, source_target_pairs={{0,4},{4,0},{8,12},{12,8},{16,20},{20,16},{24,28},{28,24},{1,5},{5... | collective-permute-start | bytes 368648 | tf_op jit(solution)/shard_map/ppermute | solution.py:191
  90.7 18.4 %collective-permute-start.8 = (bf16[3,32,640]{2,1,0:T(8,128)(2,1)S(1)}, bf16[3,32,640]{2,1,0:T(8,128)(2,1)S(1)}, u32[]{:S(2)}, u32[]{:S(2)}) collective-permute-start(bf16[3,32,640]{2,1,0:T(8,128)(2,1)S(1)} %get-tuple-element.93), channel_id=1, source_target_pairs={{0,1},{1,0},{2,3},{3,2},{4,5},{5,4},{6,7},{7,6},{8,9},{9,8},{10,11... | collective-permute-start | bytes 368648 | tf_op jit(solution)/shard_map/ppermute | solution.py:191
  109.1 21.0 %collective-permute-start.22 = (bf16[3,32,1152]{2,1,0:T(8,128)(2,1)S(1)}, bf16[3,32,1152]{2,1,0:T(8,128)(2,1)S(1)}, u32[]{:S(2)}, u32[]{:S(2)}) collective-permute-start(bf16[3,32,1152]{2,1,0:T(8,128)(2,1)S(1)} %collective-permute-done.21), channel_id=1, source_target_pairs={{0,8},{4,12},{8,0},{12,4},{16,24},{20,28},{24,16},{28,20},{1,9},{5... | collective-permute-start | bytes 663560 | tf_op jit(solution)/shard_map/ppermute | solution.py:191
  110.6 19.5 %collective-permute-start.24 = (bf16[3,32,1152]{2,1,0:T(8,128)(2,1)S(1)}, bf16[3,32,1152]{2,1,0:T(8,128)(2,1)S(1)}, u32[]{:S(2)}, u32[]{:S(2)}) collective-permute-start(bf16[3,32,1152]{2,1,0:T(8,128)(2,1)S(1)} %collective-permute-done.23), channel_id=1, source_target_pairs={{0,12},{4,8},{8,4},{12,0},{16,28},{20,24},{24,20},{28,16},{1,13},{... | collective-permute-start | bytes 663560 | tf_op jit(solution)/shard_map/ppermute | solution.py:191
  131.3 18.8 %collective-permute-start.49 = (bf16[3,32,1152]{2,1,0:T(8,128)(2,1)S(1)}, bf16[3,32,1152]{2,1,0:T(8,128)(2,1)S(1)}, u32[]{:S(2)}, u32[]{:S(2)}) collective-permute-start(bf16[3,32,1152]{2,1,0:T(8,128)(2,1)S(1)} %get-tuple-element.125), channel_id=1, source_target_pairs={{0,12},{4,8},{8,4},{12,0},{16,28},{20,24},{24,20},{28,16},{1,13},{... | collective-permute-start | bytes 663560 | tf_op jit(solution)/shard_map/ppermute | solution.py:191
  140.6 19.0 %collective-permute-start.51 = (bf16[3,32,1152]{2,1,0:T(8,128)(2,1)S(1)}, bf16[3,32,1152]{2,1,0:T(8,128)(2,1)S(1)}, u32[]{:S(2)}, u32[]{:S(2)}) collective-permute-start(bf16[3,32,1152]{2,1,0:T(8,128)(2,1)S(1)} %get-tuple-element.127), channel_id=1, source_target_pairs={{0,20},{4,16},{8,28},{12,24},{16,4},{20,0},{24,12},{28,8},{1,21},{... | collective-permute-start | bytes 663560 | tf_op jit(solution)/shard_map/ppermute | solution.py:191
  142.7 18.8 %collective-permute-start.52 = (bf16[3,32,1152]{2,1,0:T(8,128)(2,1)S(1)}, bf16[3,32,1152]{2,1,0:T(8,128)(2,1)S(1)}, u32[]{:S(2)}, u32[]{:S(2)}) collective-permute-start(bf16[3,32,1152]{2,1,0:T(8,128)(2,1)S(1)} %get-tuple-element.128), channel_id=1, source_target_pairs={{0,24},{4,28},{8,16},{12,20},{16,8},{20,12},{24,0},{28,4},{1,25},{... | collective-permute-start | bytes 663560 | tf_op jit(solution)/shard_map/ppermute | solution.py:191
  186.2 23.3 %collective-permute-start.71 = (bf16[3,64,1152]{2,1,0:T(8,128)(2,1)S(1)}, bf16[3,64,1152]{2,1,0:T(8,128)(2,1)S(1)}, u32[]{:S(2)}, u32[]{:S(2)}) collective-permute-start(bf16[3,64,1152]{2,1,0:T(8,128)(2,1)S(1)} %get-tuple-element.151), channel_id=1, source_target_pairs={{0,1},{1,0},{2,3},{3,2},{4,5},{5,4},{6,7},{7,6},{8,9},{9,8},{10,11... | collective-permute-start | bytes 1327112 | tf_op jit(solution)/shard_map/ppermute | solution.py:191
  189.5 32.9 %collective-permute-start.72 = (bf16[3,64,1152]{2,1,0:T(8,128)(2,1)S(1)}, bf16[3,64,1152]{2,1,0:T(8,128)(2,1)S(1)}, u32[]{:S(2)}, u32[]{:S(2)}) collective-permute-start(bf16[3,64,1152]{2,1,0:T(8,128)(2,1)S(1)} %get-tuple-element.152), channel_id=1, source_target_pairs={{0,2},{1,3},{2,0},{3,1},{4,6},{5,7},{6,4},{7,5},{8,10},{9,11},{10,... | collective-permute-start | bytes 1327112 | tf_op jit(solution)/shard_map/ppermute | solution.py:191
  191.4 32.5 %collective-permute-start.73 = (bf16[3,64,1152]{2,1,0:T(8,128)(2,1)S(1)}, bf16[3,64,1152]{2,1,0:T(8,128)(2,1)S(1)}, u32[]{:S(2)}, u32[]{:S(2)}) collective-permute-start(bf16[3,64,1152]{2,1,0:T(8,128)(2,1)S(1)} %get-tuple-element.129.rest_8_), channel_id=1, source_target_pairs={{0,3},{1,2},{2,1},{3,0},{4,7},{5,6},{6,5},{7,4},{8,11},{9,10},{10,... | collective-permute-start | bytes 1327112 | tf_op jit(solution)/shard_map/ppermute | solution.py:191
  203.6 26.9 %collective-permute-start.61 = (bf16[3,64,640]{2,1,0:T(8,128)(2,1)S(1)}, bf16[3,64,640]{2,1,0:T(8,128)(2,1)S(1)}, u32[]{:S(2)}, u32[]{:S(2)}) collective-permute-start(bf16[3,64,640]{2,1,0:T(8,128)(2,1)S(1)} %get-tuple-element.141), channel_id=1, source_target_pairs={{0,1},{1,0},{2,3},{3,2},{4,5},{5,4},{6,7},{7,6},{8,9},{9,8},{10,11... | collective-permute-start | bytes 737288 | tf_op jit(solution)/shard_map/ppermute | solution.py:191
  206.0 41.7 %collective-permute-start.62 = (bf16[3,64,640]{2,1,0:T(8,128)(2,1)S(1)}, bf16[3,64,640]{2,1,0:T(8,128)(2,1)S(1)}, u32[]{:S(2)}, u32[]{:S(2)}) collective-permute-start(bf16[3,64,640]{2,1,0:T(8,128)(2,1)S(1)} %get-tuple-element.142), channel_id=1, source_target_pairs={{0,2},{1,3},{2,0},{3,1},{4,6},{5,7},{6,4},{7,5},{8,10},{9,11},{10,... | collective-permute-start | bytes 737288 | tf_op jit(solution)/shard_map/ppermute | solution.py:191
  209.5 38.2 %collective-permute-start.63 = (bf16[3,64,640]{2,1,0:T(8,128)(2,1)S(1)}, bf16[3,64,640]{2,1,0:T(8,128)(2,1)S(1)}, u32[]{:S(2)}, u32[]{:S(2)}) collective-permute-start(bf16[3,64,640]{2,1,0:T(8,128)(2,1)S(1)} %get-tuple-element.130.rest_8_), channel_id=1, source_target_pairs={{0,3},{1,2},{2,1},{3,0},{4,7},{5,6},{6,5},{7,4},{8,11},{9,10},{10,... | collective-permute-start | bytes 737288 | tf_op jit(solution)/shard_map/ppermute | solution.py:191
  (51 other events, 550.4 us)
